TPU v7x, 32 devices: a whole 2x2x4 slice. The times are simulated.
32 devices in a mesh: rows: 8 (over z, x), cols: 4 (over y, core).
Axes of the slice: x: 2, y: 2, z: 4, core: 2. Of those that a mesh axis runs over, the one named last changes fastest.
Arguments:
- left_features: bfloat16 [2, 96, 512, 256], P(None, 'rows', 'cols'), may hold values from -6 to 6
- right_features: bfloat16 [2, 96, 512, 256], P(None, 'rows', 'cols'), may hold values from -6 to 6
- conv_weight: bfloat16 [3, 3, 256, 256], replicated, may hold values from -0.125 to 0.125
- conv_bias: float32 [256], replicated, may hold values from -3 to 3
Outputs:
- pyramid_out: float32 [2, 96, 512, 480], P(None, 'rows', 'cols')
All inputs are finite; a program needn't handle non-finite values.
Results may differ from a plain program's by a relative error of at most 0.0012.
Values may be sent and summed in bfloat16 or wider, within the bound.
A program may use at most 64 MiB of HBM per device.

v0:
```python
import functools
import math

import jax
import jax.numpy as jnp
from jax import lax
from jax.experimental import pallas as pl
from jax.experimental.pallas import tpu as pltpu
from jax.sharding import PartitionSpec as P

DISP = 256
LEVELS = 4


MESH = pl.DeviceIdType.MESH
AROUND = ((-1, 0), (1, 0), (0, -1), (0, 1), (-1, -1), (-1, 1), (1, -1), (1, 1))
OPPOSITE = (1, 0, 3, 2, 7, 6, 5, 4)


def encode_kernel(
    row_count, col_count, part, images, row_edges, col_edges, corners, weight_ref, bias_ref, flip_ref,
    left_out, right_out, near, far,
    row_halo, col_halo, corner_halo, padded, send_sem, recv_sem, far_sems, own_sems, pass_sems
):
    _, batch, height, breadth, channels = images.shape
    my_row, my_col = lax.axis_index("rows"), lax.axis_index("cols")
    parts = height // part
    chunks = batch * parts

    def inside(step_row, step_col):
        row, col = my_row + step_row, my_col + step_col
        return (row >= 0) & (row < row_count) & (col >= 0) & (col < col_count)

    barrier = pltpu.get_barrier_semaphore()
    partners = AROUND + ((0, -2), (0, 2))
    for step_row, step_col in partners:

        @pl.when(inside(step_row, step_col))
        def _():
            pl.semaphore_signal(
                barrier, inc=1, device_id=(my_row + step_row, my_col + step_col), device_id_type=MESH
            )

    peers = sum(inside(*step).astype(jnp.int32) for step in partners)
    pl.semaphore_wait(barrier, peers)

    def halo(side):
        if side < 2:
            return row_edges.at[side], row_halo
        if side < 4:
            return col_edges.at[side - 2], col_halo
        return corners.at[side - 4], corner_halo

    def halo_copy(side):
        first = 0 if side < 2 else 2 if side < 4 else 4
        source, target = halo(side)
        there = OPPOSITE[side]
        return pltpu.make_async_remote_copy(
            src_ref=source, dst_ref=target.at[there - first],
            send_sem=send_sem.at[side], recv_sem=recv_sem.at[there],
            device_id=(my_row + AROUND[side][0], my_col + AROUND[side][1]), device_id_type=MESH,
        )

    for side in range(8):
        there = inside(*AROUND[side])

        @pl.when(there)
        def _():
            halo_copy(side).start()

        @pl.when(jnp.logical_not(there))
        def _():
            first = 0 if side < 2 else 2 if side < 4 else 4
            target = halo(side)[1]
            target[side - first] = jnp.zeros(target.shape[1:], target.dtype)

    has_far = my_col >= 2
    odd = lax.rem(my_col, 2) == 1
    has_near = odd | has_far

    @pl.when(jnp.logical_not(has_far))
    def _():
        far[...] = jnp.zeros_like(far)

    @pl.when(jnp.logical_not(has_near))
    def _():
        near[...] = jnp.zeros_like(near)

    for side in range(8):

        @pl.when(inside(*AROUND[OPPOSITE[side]]))
        def _():
            halo_copy(side).wait_recv()

    column = lax.broadcasted_iota(jnp.int32, (breadth, 1), 0)

    def place(image, b, line, row, before, after):
        wide = row.astype(jnp.float32)
        right = jnp.where(column == 0, before.astype(jnp.float32), pltpu.roll(wide, 1, 0))
        left = jnp.where(
            column == breadth - 1, after.astype(jnp.float32), pltpu.roll(wide, breadth - 1, 0)
        )
        padded[image, b, line] = jnp.concatenate(
            [right.astype(jnp.bfloat16), row, left.astype(jnp.bfloat16)], axis=1
        )

    def prepare(image):
        for b in range(batch):
            for edge in range(2):
                place(
                    image, b, edge * (height + 1), row_halo[edge, image, b],
                    corner_halo[2 * edge, image, b], corner_halo[2 * edge + 1, image, b],
                )

            def line(h, carry):
                place(
                    image, b, h + 1, images[image, b, h],
                    col_halo[0, image, b, h], col_halo[1, image, b, h],
                )
                return carry

            lax.fori_loop(0, height, line, 0)

    def encoded(image, b, h):
        total = bias_ref[...]
        for tap in range(3):
            window = padded[image, b, pl.ds(h + tap, part)].reshape(part * breadth, 3 * channels)
            product = jnp.dot(window, weight_ref[tap], preferred_element_type=jnp.float32)
            total = product + total
        centre = images[image, b, pl.ds(h, part)].reshape(part * breadth, channels)
        out = centre.astype(jnp.float32) + jnp.maximum(total, 0.0)
        return out.astype(jnp.bfloat16).reshape(part, breadth, channels)

    def far_copy(i):
        rows = pl.ds(i * part, part)
        return pltpu.make_async_remote_copy(
            src_ref=right_out.at[rows], dst_ref=far.at[rows],
            send_sem=far_sems.at[0, i], recv_sem=far_sems.at[1, i],
            device_id=(my_row, my_col + 2), device_id_type=MESH,
        )

    def own_copy(i):
        rows = pl.ds(i * part, part)
        return pltpu.make_async_remote_copy(
            src_ref=right_out.at[rows], dst_ref=near.at[rows],
            send_sem=own_sems.at[0, i], recv_sem=own_sems.at[1, i],
            device_id=(my_row, my_col + 1), device_id_type=MESH,
        )

    def pass_copy(i):
        rows = pl.ds(i * part, part)
        return pltpu.make_async_remote_copy(
            src_ref=far.at[rows], dst_ref=near.at[rows],
            send_sem=pass_sems.at[0, i], recv_sem=pass_sems.at[1, i],
            device_id=(my_row, my_col - 1), device_id_type=MESH,
        )

    sends_far = my_col + 2 < col_count
    even = jnp.logical_not(odd)
    prepare(1)

    def right_chunk(i, carry):
        enc = encoded(1, i // parts, (i % parts) * part)
        for row in range(part):
            turned = jnp.dot(flip_ref[...], enc[row], preferred_element_type=jnp.float32)
            right_out[i * part + row] = turned.astype(jnp.bfloat16)

        @pl.when(sends_far)
        def _():
            far_copy(i).start()

        @pl.when(even)
        def _():
            own_copy(i).start()

        return carry

    lax.fori_loop(0, chunks, right_chunk, 0)
    prepare(0)

    def left_chunk(i, carry):
        left_out[pl.ds(i * part, part)] = encoded(0, i // parts, (i % parts) * part)
        return carry

    lax.fori_loop(0, chunks, left_chunk, 0)

    def arrive(i, carry):
        @pl.when(has_far)
        def _():
            far_copy(i).wait_recv()

        @pl.when(has_far & odd)
        def _():
            pass_copy(i).start()

        return carry

    lax.fori_loop(0, chunks, arrive, 0)

    def finish(i, carry):
        @pl.when(odd)
        def _():
            own_copy(i).wait_recv()

        @pl.when(has_far & even)
        def _():
            pass_copy(i).wait_recv()

        @pl.when(has_far & odd)
        def _():
            pass_copy(i).wait_send()

        @pl.when(sends_far)
        def _():
            far_copy(i).wait_send()

        @pl.when(even)
        def _():
            own_copy(i).wait_send()

        return carry

    lax.fori_loop(0, chunks, finish, 0)
    for side in range(8):

        @pl.when(inside(*AROUND[side]))
        def _():
            halo_copy(side).wait_send()


def encode(left_features, right_features, conv_weight, conv_bias):
    batch, height, breadth, channels = left_features.shape
    images = jnp.stack([left_features, right_features])
    row_edges = jnp.stack([images[:, :, 0], images[:, :, -1]])
    col_edges = jnp.stack([images[:, :, :, :1], images[:, :, :, -1:]])
    corners = jnp.stack(
        [images[:, :, r, c : c + 1] for r in (0, height - 1) for c in (0, breadth - 1)]
    )
    weight = conv_weight.reshape(3, 3 * channels, channels)
    flip = jnp.eye(breadth, dtype=jnp.bfloat16)[::-1]
    part = math.gcd(height, 4)
    chunks = batch * height // part
    flat = jax.ShapeDtypeStruct((batch * height, breadth, channels), jnp.bfloat16)
    vmem = pl.BlockSpec(memory_space=pltpu.VMEM)
    dma = pltpu.SemaphoreType.DMA
    return pl.pallas_call(
        functools.partial(encode_kernel, lax.axis_size("rows"), lax.axis_size("cols"), part),
        out_shape=[flat] * 4,
        in_specs=[vmem] * 7,
        out_specs=[vmem] * 4,
        scratch_shapes=[
            pltpu.VMEM(row_edges.shape, jnp.bfloat16),
            pltpu.VMEM(col_edges.shape, jnp.bfloat16),
            pltpu.VMEM(corners.shape, jnp.bfloat16),
            pltpu.VMEM((2, batch, height + 2, breadth, 3 * channels), jnp.bfloat16),
            dma((8,)), dma((8,)), dma((2, chunks)), dma((2, chunks)), dma((2, chunks)),
        ],
        compiler_params=pltpu.CompilerParams(
            collective_id=0, has_side_effects=True, vmem_limit_bytes=60 * 2**20
        ),
    )(images, row_edges, col_edges, corners, weight, conv_bias.reshape(1, -1), flip)


def pooling(span_count, level_count):
    lines = []
    entry = lax.broadcasted_iota(jnp.int32, (1, span_count), 1)
    for level in range(1, level_count):
        group = lax.broadcasted_iota(jnp.int32, (span_count >> level, 1), 0)
        lines.append(jnp.where((entry >> level) == group, 0.5**level, 0.0))
    return jnp.concatenate(lines, axis=0).astype(jnp.bfloat16)


def skewed(scores, span_count, scratch):
    breadth = scores.shape[1]
    lane = lax.broadcasted_iota(jnp.int32, (1, breadth), 1)
    steps = breadth - 1 - lane
    bit = breadth // 2
    while bit >= 8:
        keep = span_count + bit
        scores = jnp.where((steps & bit) != 0, scores[bit : bit + keep], scores[:keep])
        bit //= 2
    for stage, bit in enumerate((4, 2, 1)):
        keep = span_count + (8 if bit > 1 else 0)
        scratch[stage, : span_count + 8] = scores
        scores = jnp.where((steps & bit) != 0, scratch[stage, pl.ds(bit, keep)], scores[:keep])
    return scores


def correlate_kernel(span_count, scale, left_ref, *refs):
    right_refs, pool_ref, out_ref, scratch = refs[:-3], refs[-3], refs[-2], refs[-1]
    rows = left_ref.shape[0]
    pool = pool_ref[...]
    breadth = left_ref.shape[1]
    for pair in range(0, rows, 2):
        volumes = []
        for row in range(pair, min(pair + 2, rows)):
            query = left_ref[row]
            scores = jnp.concatenate(
                [
                    lax.dot_general(
                        ref[row], query, (((1,), (1,)), ((), ())), preferred_element_type=jnp.float32
                    )
                    for ref in right_refs
                ],
                axis=0,
            )
            volume = skewed(scores, span_count, scratch.at[row]) * scale
            out_ref[row, :span_count] = volume
            volumes.append(volume)
        volume = jnp.concatenate(volumes, axis=1)
        high = volume.astype(jnp.bfloat16)
        low = (volume - high.astype(jnp.float32)).astype(jnp.bfloat16)
        pooled = jnp.dot(pool, high, preferred_element_type=jnp.float32) + jnp.dot(
            pool, low, preferred_element_type=jnp.float32
        )
        for index in range(len(volumes)):
            out_ref[pair + index, span_count:] = pooled[:, index * breadth : (index + 1) * breadth]


def correlate(left, rights, span_count, level_count, block):
    rows, breadth, channels = left.shape
    pool = pooling(span_count, level_count)
    width = span_count + pool.shape[0]
    part = pl.BlockSpec((block, breadth, channels), lambda i: (i, 0, 0))
    return pl.pallas_call(
        functools.partial(correlate_kernel, span_count, 1.0 / math.sqrt(channels)),
        grid=(rows // block,),
        out_shape=jax.ShapeDtypeStruct((rows, width, breadth), jnp.float32),
        in_specs=[part] * (1 + len(rights)) + [pl.BlockSpec(pool.shape, lambda i: (0, 0))],
        out_specs=pl.BlockSpec((block, width, breadth), lambda i: (i, 0, 0)),
        scratch_shapes=[pltpu.VMEM((block, 3, span_count + 16, breadth), jnp.float32)],
        cost_estimate=pl.CostEstimate(
            flops=2 * rows * breadth * (len(rights) * breadth * channels + 2 * span_count * 256),
            bytes_accessed=rows * breadth * (2 * channels * (1 + len(rights)) + 4 * width),
            transcendentals=0,
        ),
    )(left, *rights, pool)


def shards(left_features, right_features, conv_weight, conv_bias):
    batch, height, breadth, channels = left_features.shape
    count = lax.axis_size("cols")
    assert 2 * breadth == DISP and count % 2 == 0
    left, right, near, far = encode(left_features, right_features, conv_weight, conv_bias)
    rows_total = batch * height
    out = correlate(left, [right, near, far], DISP, LEVELS, math.gcd(rows_total, 4))
    return jnp.swapaxes(out, 1, 2).reshape(batch, height, breadth, -1)


def solution(mesh):
    return jax.shard_map(
        shards,
        mesh=mesh,
        in_specs=(P(None, "rows", "cols", None), P(None, "rows", "cols", None), P(), P()),
        out_specs=P(None, "rows", "cols", None),
        check_vma=False,
    )
```

profile of v0, /device:TPU:12, one launch (start us, length us, event | category | flops | bytes accessed | tf_op | source)
XLA Modules:
  0.0 75.5 jit_solution(4617205093562575453)
XLA Ops:
  0.0 0.0 copy-start
  0.0 0.0 copy-start.1
  0.0 1.0 %fusion.14 = (bf16[1,2,2,1,256]{4,3,2,1,0:T(2,128)(2,1)S(1)}, bf16[1,2,2,1,256]{4,3,2,1,0:T(2,128)(2,1)S(1)}, bf16[1,2,2,1,256]{4,3,2,1,0:T(2,128)(2,1)S(1)}, bf16[1,2,2,1,256]{4,3,2,1,0:T(2,128)(2,1)S(1)}) fusion(bf16[1,2,12,128,256]{4,3,2,1,0:T(8,128)(2,1)} %bitcast.23, bf16[1,2,12,128,256]{4,3,2,1,0:T(8,128)(2,1)} %bitcast.27), kind=kLoop, calls=%fused_computation.44 | loop fusion | flops 4096 | bytes 3153920 | tf_op jit(solution)/shard_map/stack;squeeze | solution.py:236
  1.0 0.6 pad_maximum_fusion.4.corners
  1.7 0.6 rev.3.flip_ref
  2.3 0.7 pad_maximum_fusion.2.refs_3_
  3.0 0.0 copy-done
  3.0 0.0 copy-done.1
  3.0 0.1 fusion.5
  3.1 0.1 copy_bitcast_fusion
  3.3 0.8 %pad_maximum_fusion.3.col_edges = bf16[2,2,2,12,1,256]{5,4,3,2,1,0:T(2,128)(2,1)} fusion(bf16[1,2,2,12,1,256]{5,4,3,2,1,0:T(2,128)(2,1)S(1)} %copy.66, bf16[1,2,2,12,1,256]{5,4,3,2,1,0:T(2,128)(2,1)S(1)} %copy.65), kind=kLoop, calls=%fused_computation.25 | loop fusion | flops 24576 | bytes 98304 | tf_op jit(solution)/shard_map/stack | solution.py:235
  4.1 0.9 %pad_maximum_fusion.1.row_edges = bf16[2,2,2,128,256]{4,3,2,1,0:T(8,128)(2,1)} fusion(bf16[1,2,2,128,256]{4,3,2,1,0:T(8,128)(2,1)S(1)} %get-tuple-element.20, bf16[1,2,2,128,256]{4,3,2,1,0:T(8,128)(2,1)S(1)} %get-tuple-element.19), kind=kLoop, calls=%fused_computation.17 | loop fusion | flops 262144 | bytes 1048576 | tf_op jit(solution)/shard_map/stack | solution.py:234
  5.0 1.9 %pad_maximum_fusion.images = bf16[2,2,12,128,256]{4,3,2,1,0:T(8,128)(2,1)} fusion(bf16[1,2,12,128,256]{4,3,2,1,0:T(8,128)(2,1)S(1)} %bitcast.26, bf16[1,2,12,128,256]{4,3,2,1,0:T(8,128)(2,1)S(1)} %bitcast.30), kind=kLoop, calls=%fused_computation.8 | loop fusion | flops 1572864 | bytes 6291456 | tf_op jit(solution)/shard_map/stack | solution.py:233
  6.9 59.3 %shard_map.46 = (bf16[24,128,256]{2,1,0:T(8,128)(2,1)}, bf16[24,128,256]{2,1,0:T(8,128)(2,1)}, bf16[24,128,256]{2,1,0:T(8,128)(2,1)}, bf16[24,128,256]{2,1,0:T(8,128)(2,1)}) custom-call(bf16[2,2,12,128,256]{4,3,2,1,0:T(8,128)(2,1)} %pad_maximum_fusion.images, bf16[2,2,2,128,256]{4,3,2,1,0:T(8,128)(2,1)} %pad_maximum_fusion.1.row_edges, ...), custom_call_target="tpu_custom_call" | custom-call | tf_op jit(solution)/shard_map/pallas_call | solution.py:246
  66.2 9.4 %shard_map.47 = f32[24,480,128]{2,1,0:T(8,128)} custom-call(bf16[24,128,256]{2,1,0:T(8,128)(2,1)} %get-tuple-element.9.left_ref, bf16[24,128,256]{2,1,0:T(8,128)(2,1)} %get-tuple-element.10.refs_0_, bf16[24,128,256]{2,1,0:T(8,128)(2,1)} %get-tuple-element.11.refs_1_, bf16[24,128,256]{2,1,0:T(8,128)(2,1)} %get-tuple-element.12.refs_2_, ...), custom_call_target="tpu_custom_call" | custom-call | flops 1409286144 | bytes 12189696 | tf_op jit(solution)/shard_map/pallas_call | solution.py:325
  (10 shorter events, 0.2 us)
Async XLA Ops:
  0.0 3.0 %copy-start = (bf16[2,12,128,256]{3,2,1,0:T(8,128)(2,1)S(1)}, bf16[2,12,128,256]{3,2,1,0:T(8,128)(2,1)}, u32[]{:S(2)}) copy-start(bf16[2,12,128,256]{3,2,1,0:T(8,128)(2,1)} %param.5) | copy-start | bytes 4718596
  0.0 3.0 %copy-start.1 = (bf16[2,12,128,256]{3,2,1,0:T(8,128)(2,1)S(1)}, bf16[2,12,128,256]{3,2,1,0:T(8,128)(2,1)}, u32[]{:S(2)}) copy-start(bf16[2,12,128,256]{3,2,1,0:T(8,128)(2,1)} %param.4) | copy-start | bytes 4718596
where the time goes:
time: 76.1 us; the launch traced here: 75.5 us
  Pallas kernels  68.6 us (90%)
  other arithmetic  6.06 us (8%)
    pallas_call x1, Pallas kernels, encode(): pl.pallas_call(functools.partial(encode_kernel, lax.axis_size('rows'), la...  59.3 us
    pallas_call x1, Pallas kernels, correlate(): pl.pallas_call(functools.partial(correlate_kernel, span_count, 1.0 / math...  9.35 us
    another operation x2, other arithmetic, encode(): images = jnp.stack([left_features, right_features])  2.05 us
    another operation x2, other arithmetic, encode(): jnp.stack([images[:, :, r, c:c + 1] for r in (0, height - 1) for c in (0,...  1.61 us

commit v1 on v0

v1 whole, which is shorter than its diff:
```python
import functools
import math

import jax
import jax.numpy as jnp
from jax import lax
from jax.experimental import pallas as pl
from jax.experimental.pallas import tpu as pltpu
from jax.sharding import PartitionSpec as P

DISP = 256
LEVELS = 4


MESH = pl.DeviceIdType.MESH
AROUND = ((-1, 0), (1, 0), (0, -1), (0, 1), (-1, -1), (-1, 1), (1, -1), (1, 1))
OPPOSITE = (1, 0, 3, 2, 7, 6, 5, 4)
ROW_SIDES = (0, 1)
COL_SIDES = (2, 3)
CORNERS = (4, 5, 6, 7)
LEFT, RIGHT = 0, 1


def kernel(
    row_count, col_count, part, span_count, level_count, scale,
    left, right, weight_hbm, bias_hbm, out,
    images, sides, edges, col_halo, weight, bias, enc, near, far, back, tri_out, tri_in, scores, stage,
    in_sems, send_sem, recv_sem, own_sems, far_sems, pass_sems, back_sems, tri_sems,
):
    batch, height, breadth, channels = left.shape
    my_row, my_col = lax.axis_index("rows"), lax.axis_index("cols")
    parts = height // part
    chunks = batch * parts
    inner = batch * max(parts - 2, 0)

    def inside(step_row, step_col):
        row, col = my_row + step_row, my_col + step_col
        return (row >= 0) & (row < row_count) & (col >= 0) & (col < col_count)

    odd = lax.rem(my_col, 2) == 1
    even = jnp.logical_not(odd)
    has_two = my_col >= 2
    gives_two = my_col + 2 < col_count
    has_near = my_col >= 1
    first = jnp.where(gives_two, RIGHT, LEFT)
    second = 1 - first

    def fetch(image):
        source = right if image == RIGHT else left
        return pltpu.make_async_copy(
            source, images.at[image, :, pl.ds(1, height)], in_sems.at[image]
        )

    def fetch_weight():
        return pltpu.make_async_copy(weight_hbm, weight, in_sems.at[2])

    def fetch_bias():
        return pltpu.make_async_copy(bias_hbm, bias, in_sems.at[3])

    for image in (RIGHT, LEFT):

        @pl.when(first == image)
        def _():
            fetch(image).start()
            fetch_weight().start()
            fetch_bias().start()
            fetch(1 - image).start()

    barrier = pltpu.get_barrier_semaphore()
    partners = AROUND + ((0, -2), (0, 2))
    for step_row, step_col in partners:

        @pl.when(inside(step_row, step_col))
        def _():
            pl.semaphore_signal(
                barrier, inc=1, device_id=(my_row + step_row, my_col + step_col), device_id_type=MESH
            )

    def halo_copy(side, image):
        step_row, step_col = AROUND[side]
        if step_col == 0:
            source = images.at[image, :, 1 if step_row < 0 else height]
            target = images.at[image, :, height + 1 if step_row < 0 else 0]
        else:
            mine, theirs = (0, 1) if step_col < 0 else (1, 0)
            if step_row == 0:
                source = edges.at[mine, image]
                target = col_halo.at[theirs, image, :, pl.ds(1, height)]
            else:
                source = edges.at[mine, image, :, 0 if step_row < 0 else height - 1]
                target = col_halo.at[theirs, image, :, height + 1 if step_row < 0 else 0]
        return pltpu.make_async_remote_copy(
            src_ref=source, dst_ref=target,
            send_sem=send_sem.at[image, side], recv_sem=recv_sem.at[image, OPPOSITE[side]],
            device_id=(my_row + step_row, my_col + step_col), device_id_type=MESH,
        )

    def take_edges(image):
        def line(i, carry):
            b, h = i // height, lax.rem(i, height)
            low = images[image, b, h + 1, 0:16].astype(jnp.float32)
            high = images[image, b, h + 1, breadth - 16 : breadth].astype(jnp.float32)
            edges[0, image, b, h] = low[0:1]
            edges[1, image, b, h] = high[15:16]
            return carry

        lax.fori_loop(0, batch * height, line, 0)

    def send_halo(which, image):
        for side in which:

            @pl.when(inside(*AROUND[side]))
            def _():
                halo_copy(side, image).start()

    def wait_halo(which, image):
        for side in which:

            @pl.when(inside(*AROUND[OPPOSITE[side]]))
            def _():
                halo_copy(side, image).wait_recv()

    def clear_halo():
        for side in range(8):
            step_row, step_col = AROUND[side]

            @pl.when(jnp.logical_not(inside(step_row, step_col)))
            def _():
                line = 0 if step_row < 0 else height + 1
                for image in (LEFT, RIGHT):
                    for b in range(batch):
                        if step_col == 0:
                            images[image, b, line] = jnp.zeros((breadth, channels), jnp.bfloat16)
                        elif step_row == 0:
                            col_halo[0 if step_col < 0 else 1, image, b, pl.ds(1, height)] = jnp.zeros(
                                (height, 1, channels), jnp.float32
                            )
                        else:
                            col_halo[0 if step_col < 0 else 1, image, b, line] = jnp.zeros(
                                (1, channels), jnp.float32
                            )

    for image in (RIGHT, LEFT):

        @pl.when(first == image)
        def _():
            fetch(image).wait()

    take_edges(first)
    peers = sum(inside(*step).astype(jnp.int32) for step in partners)
    pl.semaphore_wait(barrier, peers)
    for image in (RIGHT, LEFT):

        @pl.when(first == image)
        def _():
            send_halo(COL_SIDES + CORNERS, image)
            fetch(1 - image).wait()

    take_edges(second)
    for image in (RIGHT, LEFT):

        @pl.when(first == image)
        def _():
            send_halo(COL_SIDES + CORNERS, 1 - image)
            send_halo(ROW_SIDES, image)

    clear_halo()

    @pl.when(jnp.logical_not(has_near))
    def _():
        near[...] = jnp.zeros_like(near)

    @pl.when(jnp.logical_not(has_two))
    def _():
        scores[:, 2 * breadth :] = jnp.zeros((part, scores.shape[1] - 2 * breadth, breadth), jnp.float32)

    fetch_weight().wait()
    fetch_bias().wait()

    column = lax.broadcasted_iota(jnp.int32, (breadth, 1), 0)
    flip = jnp.where(
        lax.broadcasted_iota(jnp.int32, (breadth, breadth), 0)
        + lax.broadcasted_iota(jnp.int32, (breadth, breadth), 1)
        == breadth - 1,
        1.0, 0.0,
    ).astype(jnp.bfloat16)

    def place_of(step):
        after = step - inner
        is_inner = step < inner
        span = max(parts - 2, 1)
        b = jnp.where(is_inner, step // span, lax.rem(jnp.maximum(after, 0), batch))
        c = jnp.where(
            is_inner, 1 + lax.rem(step, span), (jnp.maximum(after, 0) // batch) * (parts - 1)
        )
        return b, c * part

    def chunk(step):
        b, h = place_of(step)
        return pl.ds(b * height + h, part)

    def remote(source, target, sems, step, away):
        return pltpu.make_async_remote_copy(
            src_ref=source.at[chunk(step)], dst_ref=target.at[chunk(step)],
            send_sem=sems.at[0, step], recv_sem=sems.at[1, step],
            device_id=(my_row, my_col + away), device_id_type=MESH,
        )

    def own_copy(step):
        return remote(enc.at[RIGHT], near, own_sems, step, 1)

    def far_copy(step):
        return remote(enc.at[RIGHT], far, far_sems, step, 2)

    def pass_copy(step):
        return remote(far, near, pass_sems, step, -1)

    def back_copy(step):
        return remote(enc.at[LEFT], back, back_sems, step, -2)

    def tri_copy(step):
        return remote(tri_out, tri_in, tri_sems, step, 2)

    def convolve(image, step):
        b, h = place_of(step)
        for line in range(part + 2):
            row = images[image, b, h + line].astype(jnp.float32)
            before = col_halo[0, image, b, h + line]
            after = col_halo[1, image, b, h + line]
            sides[line, :, :channels] = jnp.where(
                column == 0, before, pltpu.roll(row, 1, 0)
            ).astype(jnp.bfloat16)
            sides[line, :, channels:] = jnp.where(
                column == breadth - 1, after, pltpu.roll(row, breadth - 1, 0)
            ).astype(jnp.bfloat16)
        pieces = []
        for tap in range(3):
            beside = sides[tap : tap + part].reshape(part * breadth, 2 * channels)
            centre = images[image, b, pl.ds(h + tap, part)].reshape(part * breadth, channels)
            pieces += [beside[:, :channels], centre, beside[:, channels:]]
        total = jnp.dot(
            jnp.concatenate(pieces, axis=1), weight[...], preferred_element_type=jnp.float32
        ) + bias[...]
        centre = images[image, b, pl.ds(h + 1, part)].reshape(part * breadth, channels)
        result = centre.astype(jnp.float32) + jnp.maximum(total, 0.0)
        result = result.astype(jnp.bfloat16).reshape(part, breadth, channels)
        base = b * height + h

        @pl.when(image == LEFT)
        def _():
            enc[LEFT, pl.ds(base, part)] = result

            @pl.when(even & has_two)
            def _():
                back_copy(step).start()

        @pl.when(image == RIGHT)
        def _():
            for row in range(part):
                turned = jnp.dot(flip, result[row], preferred_element_type=jnp.float32)
                enc[RIGHT, base + row] = turned.astype(jnp.bfloat16)

            @pl.when(even)
            def _():
                own_copy(step).start()

            @pl.when(odd & gives_two)
            def _():
                far_copy(step).start()

    def conv_loop(image, low, high):
        def body(step, carry):
            convolve(image, step)
            return carry

        lax.fori_loop(low, high, body, 0)

    def both(act, image):
        for choice in (RIGHT, LEFT):

            @pl.when(image == choice)
            def _():
                act(choice)

    both(functools.partial(wait_halo, COL_SIDES), first)
    if inner:
        conv_loop(first, 0, inner)
    both(functools.partial(wait_halo, ROW_SIDES + CORNERS), first)
    both(functools.partial(send_halo, ROW_SIDES), second)
    conv_loop(first, inner, chunks)
    both(functools.partial(wait_halo, COL_SIDES), second)
    if inner:
        conv_loop(second, 0, inner)
    both(functools.partial(wait_halo, ROW_SIDES + CORNERS), second)
    conv_loop(second, inner, chunks)

    def product(keys, queries):
        return lax.dot_general(
            keys, queries, (((1,), (1,)), ((), ())), preferred_element_type=jnp.float32
        )

    blocks = breadth // 8
    lane8 = lax.broadcasted_iota(jnp.int32, (8, breadth), 1)

    def triangle(step, carry):
        b, h = place_of(step)
        base = b * height + h
        back_copy(step).wait_recv()
        for row in range(part):
            block = product(enc[RIGHT, base + row], back[base + row])
            tri_out[base + row, 0:8] = block[0:8]
            for i in range(1, blocks // 2):
                cut = breadth - 8 * i
                tri_out[base + row, 8 * i : 8 * i + 8] = jnp.where(
                    lane8 < cut, block[8 * i : 8 * i + 8], pltpu.roll(block[cut : cut + 8], cut, 1)
                )
            tri_out[base + row, breadth // 2 :] = block[breadth // 2 : breadth // 2 + 8]
        tri_copy(step).start()
        return carry

    @pl.when(even & gives_two)
    def _():
        lax.fori_loop(0, chunks, triangle, 0)

    steps_right = breadth - 1 - lax.broadcasted_iota(jnp.int32, (1, breadth), 1)

    def volume_row(slot, line):
        bit = breadth // 2
        keep = span_count + bit
        value = None
        while bit >= 8:
            keep = span_count + bit
            if value is None:
                low, high = scores[slot, :keep], scores[slot, bit : bit + keep]
            else:
                low, high = value[:keep], value[bit : bit + keep]
            value = jnp.where((steps_right & bit) != 0, high, low)
            bit //= 2
        for index, bit in enumerate((4, 2, 1)):
            keep = span_count + (8 if bit > 1 else 0)
            stage[slot, index, : span_count + 8] = value
            value = jnp.where(
                (steps_right & bit) != 0, stage[slot, index, pl.ds(bit, keep)], value[:keep]
            )
        out[line, :span_count] = value * scale
        start, size = 0, span_count
        for _ in range(1, level_count):
            half = size // 2
            pooled = (
                out[line, pl.ds(start, half, stride=2)] + out[line, pl.ds(start + 1, half, stride=2)]
            ) * 0.5
            start, size = start + size, half
            out[line, start : start + half] = pooled

    def finish(step, carry):
        b, h = place_of(step)
        base = b * height + h

        @pl.when(odd)
        def _():
            own_copy(step).wait_recv()

        @pl.when(odd & has_two)
        def _():
            far_copy(step).wait_recv()
            pass_copy(step).start()
            for row in range(part):
                scores[row, 2 * breadth : 3 * breadth] = product(
                    far[base + row], enc[LEFT, base + row]
                )

        @pl.when(even & has_two)
        def _():
            pass_copy(step).wait_recv()
            tri_copy(step).wait_recv()
            for row in range(part):
                for i in range(blocks // 2 + 1):
                    block = tri_in[base + row, 8 * i : 8 * i + 8]
                    scores[row, 2 * breadth + 8 * i : 2 * breadth + 8 * i + 8] = block
                    if 0 < i < blocks // 2:
                        cut = breadth - 8 * i
                        scores[row, 2 * breadth + cut : 2 * breadth + cut + 8] = pltpu.roll(
                            block, 8 * i, 1
                        )

        for row in range(part):
            scores[row, :breadth] = product(enc[RIGHT, base + row], enc[LEFT, base + row])
            scores[row, breadth : 2 * breadth] = product(near[base + row], enc[LEFT, base + row])
            volume_row(row, base + row)
        return carry

    lax.fori_loop(0, chunks, finish, 0)

    def drain(step, carry):
        @pl.when(even)
        def _():
            own_copy(step).wait_send()

        @pl.when(odd & gives_two)
        def _():
            far_copy(step).wait_send()

        @pl.when(odd & has_two)
        def _():
            pass_copy(step).wait_send()

        @pl.when(even & has_two)
        def _():
            back_copy(step).wait_send()

        @pl.when(even & gives_two)
        def _():
            tri_copy(step).wait_send()

        return carry

    lax.fori_loop(0, chunks, drain, 0)
    for side in range(8):

        @pl.when(inside(*AROUND[side]))
        def _():
            for image in (LEFT, RIGHT):
                halo_copy(side, image).wait_send()


def in_hbm(array):
    return pltpu.with_memory_space_constraint(array, pltpu.HBM)


def shards(left_features, right_features, conv_weight, conv_bias):
    batch, height, breadth, channels = left_features.shape
    col_count = lax.axis_size("cols")
    assert 2 * breadth == DISP and col_count % 2 == 0 and breadth % 16 == 0
    part = math.gcd(height, 4)
    lines = batch * height
    chunks = lines // part
    width = sum(DISP >> level for level in range(LEVELS))
    hbm = pl.BlockSpec(memory_space=pltpu.HBM)
    vmem = pl.BlockSpec(memory_space=pltpu.VMEM)
    dma = pltpu.SemaphoreType.DMA
    bf16, f32 = jnp.bfloat16, jnp.float32
    tri_rows = breadth // 2 + 8
    out = pl.pallas_call(
        functools.partial(
            kernel, lax.axis_size("rows"), col_count, part, DISP, LEVELS, 1.0 / math.sqrt(channels)
        ),
        out_shape=jax.ShapeDtypeStruct((lines, width, breadth), f32),
        in_specs=[hbm] * 4,
        out_specs=vmem,
        scratch_shapes=[
            pltpu.VMEM((2, batch, height + 2, breadth, channels), bf16),
            pltpu.VMEM((part + 2, breadth, 2 * channels), bf16),
            pltpu.VMEM((2, 2, batch, height, 1, channels), f32),
            pltpu.VMEM((2, 2, batch, height + 2, 1, channels), f32),
            pltpu.VMEM((9 * channels, channels), bf16),
            pltpu.VMEM((1, channels), f32),
            pltpu.VMEM((2, lines, breadth, channels), bf16),
            pltpu.VMEM((lines, breadth, channels), bf16),
            pltpu.VMEM((lines, breadth, channels), bf16),
            pltpu.VMEM((lines, breadth, channels), bf16),
            pltpu.VMEM((lines, tri_rows, breadth), f32),
            pltpu.VMEM((lines, tri_rows, breadth), f32),
            pltpu.VMEM((part, 3 * breadth, breadth), f32),
            pltpu.VMEM((part, 3, DISP + 16, breadth), f32),
            dma((4,)), dma((2, 8)), dma((2, 8)),
            dma((2, chunks)), dma((2, chunks)), dma((2, chunks)), dma((2, chunks)), dma((2, chunks)),
        ],
        compiler_params=pltpu.CompilerParams(
            collective_id=0, has_side_effects=True, vmem_limit_bytes=40 * 2**20
        ),
    )(
        in_hbm(left_features), in_hbm(right_features),
        in_hbm(conv_weight.reshape(9 * channels, channels)), in_hbm(conv_bias.reshape(1, -1)),
    )
    return jnp.swapaxes(out, 1, 2).reshape(batch, height, breadth, -1)


def solution(mesh):
    return jax.shard_map(
        shards,
        mesh=mesh,
        in_specs=(P(None, "rows", "cols", None), P(None, "rows", "cols", None), P(), P()),
        out_specs=P(None, "rows", "cols", None),
        check_vma=False,
    )
```

time: 76.1 us -> 39.2 us (0.52)
  Pallas kernels: 68.6 us -> 36.4 us
  other arithmetic: 6.06 us -> 0 us
  local copies, waits for them, and re-layouts: 0.76 us -> 2.58 us
    pallas_call x2 -> x1, Pallas kernels: 68.6 us -> 36.4 us  [shards(): pl.pallas_call(functools.partial(kernel, lax.axis_size('rows'), col_count...]
    another operation x10 -> x0, other arithmetic: 5.38 us -> none  [the longest x2 2.05 us: encode(): images = jnp.stack([left_features, right_features])]
    unnamed x4 -> x1, local copies, waits for them, and re-layouts: 0.01 us -> 2.58 us
where the time goes in v1:
time: 39.2 us; the launch traced here: 39 us
  Pallas kernels  36.4 us (93%)
  local copies, waits for them, and re-layouts  2.58 us (7%)
    pallas_call x1, Pallas kernels, shards(): pl.pallas_call(functools.partial(kernel, lax.axis_size('rows'), col_count...  36.4 us
    unnamed x1, local copies, waits for them, and re-layouts  2.58 us

profile of v1, /device:TPU:12, one launch (start us, length us, event | category | flops | bytes accessed | tf_op | source)
XLA Modules:
  0.0 39.0 jit_solution(6834369842054590450)
XLA Ops:
  0.0 36.4 %shard_map.46 = f32[24,480,128]{2,1,0:T(8,128)S(1)} custom-call(bf16[2,12,128,256]{3,2,1,0:T(8,128)(2,1)} %left.1, bf16[2,12,128,256]{3,2,1,0:T(8,128)(2,1)} %right.1, bf16[2304,256]{1,0:T(8,128)(2,1)} %bitcast.6, f32[1,256]{1,0:T(1,128)} %bitcast.7), custom_call_target="tpu_custom_call" | custom-call | tf_op jit(solution)/shard_map/pallas_call | solution.py:443
  36.4 2.6 %copy.6 = f32[2,12,128,480]{2,3,1,0:T(8,128)} copy(f32[2,12,128,480]{2,3,1,0:T(8,128)S(1)} %bitcast.5) | data formatting | bytes 11796480

commit v2 on v1

--- a/solution.py
+++ b/solution.py
@@ -24,14 +24,15 @@
 def kernel(
     row_count, col_count, part, span_count, level_count, scale,
     left, right, weight_hbm, bias_hbm, out,
-    images, sides, edges, col_halo, weight, bias, enc, near, far, back, tri_out, tri_in, scores, stage,
-    in_sems, send_sem, recv_sem, own_sems, far_sems, pass_sems, back_sems, tri_sems,
+    images, sides, raw_edges, edges, col_halo, weight, bias, enc, near, far, back, tri_out, tri_in, scores, stage,
+    in_sems, edge_sems, send_sem, recv_sem, own_sems, far_sems, pass_sems, back_sems, tri_sems,
 ):
     batch, height, breadth, channels = left.shape
     my_row, my_col = lax.axis_index("rows"), lax.axis_index("cols")
-    parts = height // part
-    chunks = batch * parts
-    inner = batch * max(parts - 2, 0)
+    edge = part // 2
+    spans = height // part - 1
+    chunks = batch * (spans + 1)
+    inner = batch * spans
 
     def inside(step_row, step_col):
         row, col = my_row + step_row, my_col + step_col
@@ -51,30 +52,40 @@
             source, images.at[image, :, pl.ds(1, height)], in_sems.at[image]
         )
 
+    def fetch_edge(side, image):
+        source = right if image == RIGHT else left
+        return pltpu.make_async_copy(
+            source.at[:, :, pl.ds(side * (breadth - 16), 16)],
+            raw_edges.at[side, image], edge_sems.at[side, image],
+        )
+
     def fetch_weight():
         return pltpu.make_async_copy(weight_hbm, weight, in_sems.at[2])
 
     def fetch_bias():
         return pltpu.make_async_copy(bias_hbm, bias, in_sems.at[3])
 
+    barrier = pltpu.get_barrier_semaphore()
+    partners = AROUND + ((0, -2), (0, 2))
+    for step_row, step_col in partners:
+
+        @pl.when(inside(step_row, step_col))
+        def _():
+            pl.semaphore_signal(
+                barrier, inc=1, device_id=(my_row + step_row, my_col + step_col), device_id_type=MESH
+            )
+
     for image in (RIGHT, LEFT):
 
         @pl.when(first == image)
         def _():
+            for choice in (image, 1 - image):
+                for side in range(2):
+                    fetch_edge(side, choice).start()
             fetch(image).start()
             fetch_weight().start()
             fetch_bias().start()
             fetch(1 - image).start()
-
-    barrier = pltpu.get_barrier_semaphore()
-    partners = AROUND + ((0, -2), (0, 2))
-    for step_row, step_col in partners:
-
-        @pl.when(inside(step_row, step_col))
-        def _():
-            pl.semaphore_signal(
-                barrier, inc=1, device_id=(my_row + step_row, my_col + step_col), device_id_type=MESH
-            )
 
     def halo_copy(side, image):
         step_row, step_col = AROUND[side]
@@ -98,10 +109,8 @@
     def take_edges(image):
         def line(i, carry):
             b, h = i // height, lax.rem(i, height)
-            low = images[image, b, h + 1, 0:16].astype(jnp.float32)
-            high = images[image, b, h + 1, breadth - 16 : breadth].astype(jnp.float32)
-            edges[0, image, b, h] = low[0:1]
-            edges[1, image, b, h] = high[15:16]
+            edges[0, image, b, h] = raw_edges[0, image, b, h].astype(jnp.float32)[0:1]
+            edges[1, image, b, h] = raw_edges[1, image, b, h].astype(jnp.float32)[15:16]
             return carry
 
         lax.fori_loop(0, batch * height, line, 0)
@@ -144,7 +153,8 @@
 
         @pl.when(first == image)
         def _():
-            fetch(image).wait()
+            for side in range(2):
+                fetch_edge(side, image).wait()
 
     take_edges(first)
     peers = sum(inside(*step).astype(jnp.int32) for step in partners)
@@ -154,7 +164,8 @@
         @pl.when(first == image)
         def _():
             send_halo(COL_SIDES + CORNERS, image)
-            fetch(1 - image).wait()
+            for side in range(2):
+                fetch_edge(side, 1 - image).wait()
 
     take_edges(second)
     for image in (RIGHT, LEFT):
@@ -162,7 +173,10 @@
         @pl.when(first == image)
         def _():
             send_halo(COL_SIDES + CORNERS, 1 - image)
+            fetch(image).wait()
             send_halo(ROW_SIDES, image)
+            fetch(1 - image).wait()
+            send_halo(ROW_SIDES, 1 - image)
 
     clear_halo()
 
@@ -185,23 +199,20 @@
         1.0, 0.0,
     ).astype(jnp.bfloat16)
 
-    def place_of(step):
-        after = step - inner
+    def place_of(step, row):
         is_inner = step < inner
-        span = max(parts - 2, 1)
-        b = jnp.where(is_inner, step // span, lax.rem(jnp.maximum(after, 0), batch))
-        c = jnp.where(
-            is_inner, 1 + lax.rem(step, span), (jnp.maximum(after, 0) // batch) * (parts - 1)
+        b = jnp.where(is_inner, step // spans, step - inner)
+        h = jnp.where(
+            is_inner,
+            edge + lax.rem(step, spans) * part + row,
+            row if row < edge else height - part + row,
         )
-        return b, c * part
-
-    def chunk(step):
-        b, h = place_of(step)
-        return pl.ds(b * height + h, part)
-
-    def remote(source, target, sems, step, away):
+        return b, h
+
+    def remote(source, target, sems, step, away, rows=part):
+        lines = pl.ds(step * rows, rows)
         return pltpu.make_async_remote_copy(
-            src_ref=source.at[chunk(step)], dst_ref=target.at[chunk(step)],
+            src_ref=source.at[lines], dst_ref=target.at[lines],
             send_sem=sems.at[0, step], recv_sem=sems.at[1, step],
             device_id=(my_row, my_col + away), device_id_type=MESH,
         )
@@ -219,32 +230,38 @@
         return remote(enc.at[LEFT], back, back_sems, step, -2)
 
     def tri_copy(step):
-        return remote(tri_out, tri_in, tri_sems, step, 2)
-
-    def convolve(image, step):
-        b, h = place_of(step)
-        for line in range(part + 2):
-            row = images[image, b, h + line].astype(jnp.float32)
-            before = col_halo[0, image, b, h + line]
-            after = col_halo[1, image, b, h + line]
-            sides[line, :, :channels] = jnp.where(
-                column == 0, before, pltpu.roll(row, 1, 0)
-            ).astype(jnp.bfloat16)
-            sides[line, :, channels:] = jnp.where(
-                column == breadth - 1, after, pltpu.roll(row, breadth - 1, 0)
-            ).astype(jnp.bfloat16)
+        return remote(tri_out, tri_in, tri_sems, step, 2, part // 2)
+
+    def convolve(image, step, b, starts, count):
+        slots = count + 2
+        for piece, start in enumerate(starts):
+            for line in range(slots):
+                row = images[image, b, start + line].astype(jnp.float32)
+                before = col_halo[0, image, b, start + line]
+                after = col_halo[1, image, b, start + line]
+                sides[piece * slots + line, :, :channels] = jnp.where(
+                    column == 0, before, pltpu.roll(row, 1, 0)
+                ).astype(jnp.bfloat16)
+                sides[piece * slots + line, :, channels:] = jnp.where(
+                    column == breadth - 1, after, pltpu.roll(row, breadth - 1, 0)
+                ).astype(jnp.bfloat16)
+
+        def rows_from(offset):
+            taken = [images[image, b, pl.ds(start + offset, count)] for start in starts]
+            return jnp.concatenate(taken, axis=0).reshape(part * breadth, channels)
+
         pieces = []
         for tap in range(3):
-            beside = sides[tap : tap + part].reshape(part * breadth, 2 * channels)
-            centre = images[image, b, pl.ds(h + tap, part)].reshape(part * breadth, channels)
-            pieces += [beside[:, :channels], centre, beside[:, channels:]]
+            beside = jnp.concatenate(
+                [sides[i * slots + tap : i * slots + tap + count] for i in range(len(starts))], axis=0
+            ).reshape(part * breadth, 2 * channels)
+            pieces += [beside[:, :channels], rows_from(tap), beside[:, channels:]]
         total = jnp.dot(
             jnp.concatenate(pieces, axis=1), weight[...], preferred_element_type=jnp.float32
         ) + bias[...]
-        centre = images[image, b, pl.ds(h + 1, part)].reshape(part * breadth, channels)
-        result = centre.astype(jnp.float32) + jnp.maximum(total, 0.0)
+        result = rows_from(1).astype(jnp.float32) + jnp.maximum(total, 0.0)
         result = result.astype(jnp.bfloat16).reshape(part, breadth, channels)
-        base = b * height + h
+        base = step * part
 
         @pl.when(image == LEFT)
         def _():
@@ -268,12 +285,19 @@
             def _():
                 far_copy(step).start()
 
-    def conv_loop(image, low, high):
+    def conv_inner(image):
         def body(step, carry):
-            convolve(image, step)
+            convolve(image, step, step // spans, [edge + lax.rem(step, spans) * part], part)
             return carry
 
-        lax.fori_loop(low, high, body, 0)
+        lax.fori_loop(0, inner, body, 0)
+
+    def conv_edge(image):
+        def body(step, carry):
+            convolve(image, step, step - inner, [0, height - edge], edge)
+            return carry
+
+        lax.fori_loop(inner, chunks, body, 0)
 
     def both(act, image):
         for choice in (RIGHT, LEFT):
@@ -281,46 +305,47 @@
             @pl.when(image == choice)
             def _():
                 act(choice)
-
-    both(functools.partial(wait_halo, COL_SIDES), first)
-    if inner:
-        conv_loop(first, 0, inner)
-    both(functools.partial(wait_halo, ROW_SIDES + CORNERS), first)
-    both(functools.partial(send_halo, ROW_SIDES), second)
-    conv_loop(first, inner, chunks)
-    both(functools.partial(wait_halo, COL_SIDES), second)
-    if inner:
-        conv_loop(second, 0, inner)
-    both(functools.partial(wait_halo, ROW_SIDES + CORNERS), second)
-    conv_loop(second, inner, chunks)
 
     def product(keys, queries):
         return lax.dot_general(
             keys, queries, (((1,), (1,)), ((), ())), preferred_element_type=jnp.float32
         )
 
-    blocks = breadth // 8
+    half_blocks = breadth // 16
     lane8 = lax.broadcasted_iota(jnp.int32, (8, breadth), 1)
 
     def triangle(step, carry):
-        b, h = place_of(step)
-        base = b * height + h
+        base = step * part
         back_copy(step).wait_recv()
-        for row in range(part):
-            block = product(enc[RIGHT, base + row], back[base + row])
-            tri_out[base + row, 0:8] = block[0:8]
-            for i in range(1, blocks // 2):
+        for pair in range(0, part, 2):
+            two = [product(enc[RIGHT, base + row], back[base + row]) for row in (pair, pair + 1)]
+            for i in range(half_blocks + 1):
                 cut = breadth - 8 * i
-                tri_out[base + row, 8 * i : 8 * i + 8] = jnp.where(
-                    lane8 < cut, block[8 * i : 8 * i + 8], pltpu.roll(block[cut : cut + 8], cut, 1)
-                )
-            tri_out[base + row, breadth // 2 :] = block[breadth // 2 : breadth // 2 + 8]
+                kept = []
+                for block in two:
+                    piece = block[8 * i : 8 * i + 8]
+                    if 0 < i < half_blocks:
+                        piece = jnp.where(lane8 < cut, piece, pltpu.roll(block[cut : cut + 8], cut, 1))
+                    kept.append(piece)
+                tri_out[(base + pair) // 2, i] = jnp.concatenate(kept, axis=0).astype(jnp.bfloat16)
         tri_copy(step).start()
         return carry
 
-    @pl.when(even & gives_two)
-    def _():
-        lax.fori_loop(0, chunks, triangle, 0)
+    def triangles(low, high):
+        @pl.when(even & gives_two)
+        def _():
+            lax.fori_loop(low, high, triangle, 0)
+
+    both(functools.partial(wait_halo, COL_SIDES), first)
+    conv_inner(first)
+    both(functools.partial(wait_halo, COL_SIDES), second)
+    conv_inner(second)
+    both(functools.partial(wait_halo, ROW_SIDES + CORNERS), first)
+    conv_edge(first)
+    triangles(0, inner)
+    both(functools.partial(wait_halo, ROW_SIDES + CORNERS), second)
+    conv_edge(second)
+    triangles(inner, chunks)
 
     steps_right = breadth - 1 - lax.broadcasted_iota(jnp.int32, (1, breadth), 1)
 
@@ -353,8 +378,7 @@
             out[line, start : start + half] = pooled
 
     def finish(step, carry):
-        b, h = place_of(step)
-        base = b * height + h
+        base = step * part
 
         @pl.when(odd)
         def _():
@@ -373,20 +397,22 @@
         def _():
             pass_copy(step).wait_recv()
             tri_copy(step).wait_recv()
-            for row in range(part):
-                for i in range(blocks // 2 + 1):
-                    block = tri_in[base + row, 8 * i : 8 * i + 8]
-                    scores[row, 2 * breadth + 8 * i : 2 * breadth + 8 * i + 8] = block
-                    if 0 < i < blocks // 2:
-                        cut = breadth - 8 * i
-                        scores[row, 2 * breadth + cut : 2 * breadth + cut + 8] = pltpu.roll(
-                            block, 8 * i, 1
-                        )
+            for pair in range(0, part, 2):
+                for i in range(half_blocks + 1):
+                    both_rows = tri_in[(base + pair) // 2, i].astype(jnp.float32)
+                    for row in range(2):
+                        block = both_rows[8 * row : 8 * row + 8]
+                        start = 2 * breadth + 8 * i
+                        scores[pair + row, start : start + 8] = block
+                        if 0 < i < half_blocks:
+                            start = 3 * breadth - 8 * i
+                            scores[pair + row, start : start + 8] = pltpu.roll(block, 8 * i, 1)
 
         for row in range(part):
             scores[row, :breadth] = product(enc[RIGHT, base + row], enc[LEFT, base + row])
             scores[row, breadth : 2 * breadth] = product(near[base + row], enc[LEFT, base + row])
-            volume_row(row, base + row)
+            b, h = place_of(step, row)
+            volume_row(row, b * height + h)
         return carry
 
     lax.fori_loop(0, chunks, finish, 0)
@@ -430,8 +456,9 @@
 def shards(left_features, right_features, conv_weight, conv_bias):
     batch, height, breadth, channels = left_features.shape
     col_count = lax.axis_size("cols")
+    part = math.gcd(height, 4)
     assert 2 * breadth == DISP and col_count % 2 == 0 and breadth % 16 == 0
-    part = math.gcd(height, 4)
+    assert part % 2 == 0 and height > part
     lines = batch * height
     chunks = lines // part
     width = sum(DISP >> level for level in range(LEVELS))
@@ -439,7 +466,7 @@
     vmem = pl.BlockSpec(memory_space=pltpu.VMEM)
     dma = pltpu.SemaphoreType.DMA
     bf16, f32 = jnp.bfloat16, jnp.float32
-    tri_rows = breadth // 2 + 8
+    tri = (lines // 2, breadth // 16 + 1, 16, breadth)
     out = pl.pallas_call(
         functools.partial(
             kernel, lax.axis_size("rows"), col_count, part, DISP, LEVELS, 1.0 / math.sqrt(channels)
@@ -449,7 +476,8 @@
         out_specs=vmem,
         scratch_shapes=[
             pltpu.VMEM((2, batch, height + 2, breadth, channels), bf16),
-            pltpu.VMEM((part + 2, breadth, 2 * channels), bf16),
+            pltpu.VMEM((part + 4, breadth, 2 * channels), bf16),
+            pltpu.VMEM((2, 2, batch, height, 16, channels), bf16),
             pltpu.VMEM((2, 2, batch, height, 1, channels), f32),
             pltpu.VMEM((2, 2, batch, height + 2, 1, channels), f32),
             pltpu.VMEM((9 * channels, channels), bf16),
@@ -458,11 +486,11 @@
             pltpu.VMEM((lines, breadth, channels), bf16),
             pltpu.VMEM((lines, breadth, channels), bf16),
             pltpu.VMEM((lines, breadth, channels), bf16),
-            pltpu.VMEM((lines, tri_rows, breadth), f32),
-            pltpu.VMEM((lines, tri_rows, breadth), f32),
+            pltpu.VMEM(tri, bf16),
+            pltpu.VMEM(tri, bf16),
             pltpu.VMEM((part, 3 * breadth, breadth), f32),
             pltpu.VMEM((part, 3, DISP + 16, breadth), f32),
-            dma((4,)), dma((2, 8)), dma((2, 8)),
+            dma((4,)), dma((2, 2)), dma((2, 8)), dma((2, 8)),
             dma((2, chunks)), dma((2, chunks)), dma((2, chunks)), dma((2, chunks)), dma((2, chunks)),
         ],
         compiler_params=pltpu.CompilerParams(

time: 39.2 us -> 35.2 us (0.90)
  Pallas kernels: 36.4 us -> 32.5 us
    pallas_call x1, Pallas kernels: 36.4 us -> 32.5 us  [shards(): pl.pallas_call(functools.partial(kernel, lax.axis_size('rows'), col_count...]
where the time goes in v2:
time: 35.2 us; the launch traced here: 35.1 us
  Pallas kernels  32.5 us (92%)
  local copies, waits for them, and re-layouts  2.58 us (7%)
    pallas_call x1, Pallas kernels, shards(): pl.pallas_call(functools.partial(kernel, lax.axis_size('rows'), col_count...  32.5 us
    unnamed x1, local copies, waits for them, and re-layouts  2.58 us

profile of v2, /device:TPU:12, one launch (start us, length us, event | category | flops | bytes accessed | tf_op | source)
XLA Modules:
  0.0 35.1 jit_solution(17021104705310700971)
XLA Ops:
  0.0 32.5 %shard_map.46 = f32[24,480,128]{2,1,0:T(8,128)S(1)} custom-call(bf16[2,12,128,256]{3,2,1,0:T(8,128)(2,1)} %left.1, bf16[2,12,128,256]{3,2,1,0:T(8,128)(2,1)} %right.1, bf16[2304,256]{1,0:T(8,128)(2,1)} %bitcast.6, f32[1,256]{1,0:T(1,128)} %bitcast.7), custom_call_target="tpu_custom_call" | custom-call | tf_op jit(solution)/shard_map/pallas_call | solution.py:470
  32.5 2.6 %copy.6 = f32[2,12,128,480]{2,3,1,0:T(8,128)} copy(f32[2,12,128,480]{2,3,1,0:T(8,128)S(1)} %bitcast.5) | data formatting | bytes 11796480

commit v3 on v2

--- a/solution.py
+++ b/solution.py
@@ -18,14 +18,42 @@
 ROW_SIDES = (0, 1)
 COL_SIDES = (2, 3)
 CORNERS = (4, 5, 6, 7)
-LEFT, RIGHT = 0, 1
+LEFT, RIGHT, AHEAD = 0, 1, 2
+
+
+def volume_row(scores, stage, out, slot, line, span_count, level_count, scale):
+    breadth = scores.shape[2]
+    steps = breadth - 1 - lax.broadcasted_iota(jnp.int32, (1, breadth), 1)
+    bit = breadth // 2
+    value = None
+    while bit >= 8:
+        keep = span_count + bit
+        if value is None:
+            low, high = scores[slot, :keep], scores[slot, bit : bit + keep]
+        else:
+            low, high = value[:keep], value[bit : bit + keep]
+        value = jnp.where((steps & bit) != 0, high, low)
+        bit //= 2
+    for index, bit in enumerate((4, 2, 1)):
+        keep = span_count + (8 if bit > 1 else 0)
+        stage[slot, index, : span_count + 8] = value
+        value = jnp.where((steps & bit) != 0, stage[slot, index, pl.ds(bit, keep)], value[:keep])
+    out[line, :span_count] = value * scale
+    start, size = 0, span_count
+    for _ in range(1, level_count):
+        half = size // 2
+        pooled = (
+            out[line, pl.ds(start, half, stride=2)] + out[line, pl.ds(start + 1, half, stride=2)]
+        ) * 0.5
+        start, size = start + size, half
+        out[line, start : start + half] = pooled
 
 
 def kernel(
     row_count, col_count, part, span_count, level_count, scale,
-    left, right, weight_hbm, bias_hbm, out,
+    left, right, weight_hbm, bias_hbm, out, held,
     images, sides, raw_edges, edges, col_halo, weight, bias, enc, near, far, back, tri_out, tri_in, scores, stage,
-    in_sems, edge_sems, send_sem, recv_sem, own_sems, far_sems, pass_sems, back_sems, tri_sems,
+    in_sems, edge_sems, halo_sems, recv_sem, ahead_sems, send_sems, near_sems, two_sems, back_sems,
 ):
     batch, height, breadth, channels = left.shape
     my_row, my_col = lax.axis_index("rows"), lax.axis_index("cols")
@@ -102,18 +130,39 @@
                 target = col_halo.at[theirs, image, :, height + 1 if step_row < 0 else 0]
         return pltpu.make_async_remote_copy(
             src_ref=source, dst_ref=target,
-            send_sem=send_sem.at[image, side], recv_sem=recv_sem.at[image, OPPOSITE[side]],
+            send_sem=halo_sems.at[side],
+            recv_sem=recv_sem.at[image if isinstance(image, int) else 0, OPPOSITE[side]],
             device_id=(my_row + step_row, my_col + step_col), device_id_type=MESH,
         )
 
+    def ahead_copy(which, image):
+        lines = pl.ds(edge, part + 2)
+        if which == 0:
+            source, target = images.at[image, 0, lines], images.at[AHEAD, 0, lines]
+        else:
+            source, target = col_halo.at[:, image, 0, lines], col_halo.at[:, AHEAD, 0, lines]
+        return pltpu.make_async_remote_copy(
+            src_ref=source, dst_ref=target,
+            send_sem=ahead_sems.at[0, which], recv_sem=ahead_sems.at[1, which],
+            device_id=(my_row, my_col + (2 if image == RIGHT else -2)), device_id_type=MESH,
+        )
+
+    sends_ahead = ((RIGHT, odd & gives_two), (LEFT, even & has_two))
+    takes_ahead = ((RIGHT, odd & has_two), (LEFT, even & gives_two))
+
+    def send_ahead(which, image):
+        for choice, when in sends_ahead:
+            if choice == image:
+
+                @pl.when(when)
+                def _():
+                    ahead_copy(which, choice).start()
+
     def take_edges(image):
-        def line(i, carry):
-            b, h = i // height, lax.rem(i, height)
-            edges[0, image, b, h] = raw_edges[0, image, b, h].astype(jnp.float32)[0:1]
-            edges[1, image, b, h] = raw_edges[1, image, b, h].astype(jnp.float32)[15:16]
-            return carry
-
-        lax.fori_loop(0, batch * height, line, 0)
+        for b in range(batch):
+            for h in range(height):
+                edges[0, image, b, h] = raw_edges[0, image, b, h].astype(jnp.float32)[0:1]
+                edges[1, image, b, h] = raw_edges[1, image, b, h].astype(jnp.float32)[15:16]
 
     def send_halo(which, image):
         for side in which:
@@ -174,8 +223,10 @@
         def _():
             send_halo(COL_SIDES + CORNERS, 1 - image)
             fetch(image).wait()
+            send_ahead(0, image)
             send_halo(ROW_SIDES, image)
             fetch(1 - image).wait()
+            send_ahead(0, 1 - image)
             send_halo(ROW_SIDES, 1 - image)
 
     clear_halo()
@@ -186,7 +237,8 @@
 
     @pl.when(jnp.logical_not(has_two))
     def _():
-        scores[:, 2 * breadth :] = jnp.zeros((part, scores.shape[1] - 2 * breadth, breadth), jnp.float32)
+        for target in (scores, held):
+            target[:, 2 * breadth :] = jnp.zeros((part, breadth, breadth), jnp.float32)
 
     fetch_weight().wait()
     fetch_bias().wait()
@@ -209,28 +261,36 @@
         )
         return b, h
 
-    def remote(source, target, sems, step, away, rows=part):
+    def remote(source, target, send, recv, step, away, rows=part):
         lines = pl.ds(step * rows, rows)
         return pltpu.make_async_remote_copy(
             src_ref=source.at[lines], dst_ref=target.at[lines],
-            send_sem=sems.at[0, step], recv_sem=sems.at[1, step],
+            send_sem=send_sems.at[send], recv_sem=recv.at[step],
             device_id=(my_row, my_col + away), device_id_type=MESH,
         )
 
     def own_copy(step):
-        return remote(enc.at[RIGHT], near, own_sems, step, 1)
+        return remote(enc.at[RIGHT], near, 0, near_sems, step, 1)
 
     def far_copy(step):
-        return remote(enc.at[RIGHT], far, far_sems, step, 2)
+        return remote(enc.at[RIGHT], far, 0, two_sems, step, 2)
 
     def pass_copy(step):
-        return remote(far, near, pass_sems, step, -1)
+        return remote(far, near, 1, near_sems, step, -1)
 
     def back_copy(step):
-        return remote(enc.at[LEFT], back, back_sems, step, -2)
+        return remote(enc.at[LEFT], back, 1, back_sems, step, -2)
 
     def tri_copy(step):
-        return remote(tri_out, tri_in, tri_sems, step, 2, part // 2)
+        return remote(tri_out, tri_in, 2, two_sems, step, 2, part // 2)
+
+    def sent(source, target, send, first_line, away):
+        lines = pl.ds(first_line, source.shape[0] - first_line)
+        return pltpu.make_async_remote_copy(
+            src_ref=source.at[lines], dst_ref=target.at[lines],
+            send_sem=send_sems.at[send], recv_sem=near_sems.at[0],
+            device_id=(my_row, my_col + away), device_id_type=MESH,
+        )
 
     def convolve(image, step, b, starts, count):
         slots = count + 2
@@ -267,30 +327,42 @@
         def _():
             enc[LEFT, pl.ds(base, part)] = result
 
-            @pl.when(even & has_two)
+            @pl.when(even & has_two & (step > 0))
             def _():
                 back_copy(step).start()
 
+        def turned(row):
+            return jnp.dot(flip, result[row], preferred_element_type=jnp.float32).astype(jnp.bfloat16)
+
+        @pl.when((image == AHEAD) & odd)
+        def _():
+            for row in range(part):
+                far[base + row] = turned(row)
+            pass_copy(step).start()
+
+        @pl.when((image == AHEAD) & even)
+        def _():
+            back[pl.ds(base, part)] = result
+
         @pl.when(image == RIGHT)
         def _():
             for row in range(part):
-                turned = jnp.dot(flip, result[row], preferred_element_type=jnp.float32)
-                enc[RIGHT, base + row] = turned.astype(jnp.bfloat16)
+                enc[RIGHT, base + row] = turned(row)
 
             @pl.when(even)
             def _():
                 own_copy(step).start()
 
-            @pl.when(odd & gives_two)
+            @pl.when(odd & gives_two & (step > 0))
             def _():
                 far_copy(step).start()
 
-    def conv_inner(image):
+    def conv_inner(image, low, high):
         def body(step, carry):
             convolve(image, step, step // spans, [edge + lax.rem(step, spans) * part], part)
             return carry
 
-        lax.fori_loop(0, inner, body, 0)
+        lax.fori_loop(low, high, body, 0)
 
     def conv_edge(image):
         def body(step, carry):
@@ -316,7 +388,11 @@
 
     def triangle(step, carry):
         base = step * part
-        back_copy(step).wait_recv()
+
+        @pl.when(step > 0)
+        def _():
+            back_copy(step).wait_recv()
+
         for pair in range(0, part, 2):
             two = [product(enc[RIGHT, base + row], back[base + row]) for row in (pair, pair + 1)]
             for i in range(half_blocks + 1):
@@ -337,9 +413,21 @@
             lax.fori_loop(low, high, triangle, 0)
 
     both(functools.partial(wait_halo, COL_SIDES), first)
-    conv_inner(first)
+
+    both(functools.partial(send_ahead, 1), first)
+    conv_inner(first, 0, inner)
     both(functools.partial(wait_halo, COL_SIDES), second)
-    conv_inner(second)
+    both(functools.partial(send_ahead, 1), second)
+    conv_inner(second, 0, inner)
+    for choice, when in takes_ahead:
+
+        @pl.when(when)
+        def _():
+            ahead_copy(0, choice).wait_recv()
+            ahead_copy(1, choice).wait_recv()
+
+    any_ahead = (odd & has_two) | (even & gives_two)
+    conv_inner(AHEAD, 0, jnp.where(any_ahead, 1, 0))
     both(functools.partial(wait_halo, ROW_SIDES + CORNERS), first)
     conv_edge(first)
     triangles(0, inner)
@@ -347,37 +435,7 @@
     conv_edge(second)
     triangles(inner, chunks)
 
-    steps_right = breadth - 1 - lax.broadcasted_iota(jnp.int32, (1, breadth), 1)
-
-    def volume_row(slot, line):
-        bit = breadth // 2
-        keep = span_count + bit
-        value = None
-        while bit >= 8:
-            keep = span_count + bit
-            if value is None:
-                low, high = scores[slot, :keep], scores[slot, bit : bit + keep]
-            else:
-                low, high = value[:keep], value[bit : bit + keep]
-            value = jnp.where((steps_right & bit) != 0, high, low)
-            bit //= 2
-        for index, bit in enumerate((4, 2, 1)):
-            keep = span_count + (8 if bit > 1 else 0)
-            stage[slot, index, : span_count + 8] = value
-            value = jnp.where(
-                (steps_right & bit) != 0, stage[slot, index, pl.ds(bit, keep)], value[:keep]
-            )
-        out[line, :span_count] = value * scale
-        start, size = 0, span_count
-        for _ in range(1, level_count):
-            half = size // 2
-            pooled = (
-                out[line, pl.ds(start, half, stride=2)] + out[line, pl.ds(start + 1, half, stride=2)]
-            ) * 0.5
-            start, size = start + size, half
-            out[line, start : start + half] = pooled
-
-    def finish(step, carry):
+    def finish(step, scores):
         base = step * part
 
         @pl.when(odd)
@@ -386,8 +444,11 @@
 
         @pl.when(odd & has_two)
         def _():
-            far_copy(step).wait_recv()
-            pass_copy(step).start()
+            @pl.when(step > 0)
+            def _():
+                far_copy(step).wait_recv()
+                pass_copy(step).start()
+
             for row in range(part):
                 scores[row, 2 * breadth : 3 * breadth] = product(
                     far[base + row], enc[LEFT, base + row]
@@ -411,42 +472,76 @@
         for row in range(part):
             scores[row, :breadth] = product(enc[RIGHT, base + row], enc[LEFT, base + row])
             scores[row, breadth : 2 * breadth] = product(near[base + row], enc[LEFT, base + row])
-            b, h = place_of(step, row)
-            volume_row(row, b * height + h)
+            if scores is not held:
+                b, h = place_of(step, row)
+                volume_row(
+                    scores, stage, out, row, b * height + h, span_count, level_count, scale
+                )
+
+    def finish_one(step, carry):
+        finish(step, scores)
         return carry
 
-    lax.fori_loop(0, chunks, finish, 0)
-
-    def drain(step, carry):
-        @pl.when(even)
-        def _():
-            own_copy(step).wait_send()
-
-        @pl.when(odd & gives_two)
-        def _():
-            far_copy(step).wait_send()
-
-        @pl.when(odd & has_two)
-        def _():
-            pass_copy(step).wait_send()
-
-        @pl.when(even & has_two)
-        def _():
-            back_copy(step).wait_send()
-
-        @pl.when(even & gives_two)
-        def _():
-            tri_copy(step).wait_send()
-
-        return carry
-
-    lax.fori_loop(0, chunks, drain, 0)
+    lax.fori_loop(0, chunks - 1, finish_one, 0)
+
+    @pl.when(even)
+    def _():
+        sent(enc.at[RIGHT], near, 0, 0, 1).wait_send()
+
+    @pl.when(even & has_two)
+    def _():
+        sent(enc.at[LEFT], back, 1, part, -2).wait_send()
+
+    @pl.when(odd & gives_two)
+    def _():
+        sent(enc.at[RIGHT], far, 0, part, 2).wait_send()
+
+    for choice, when in sends_ahead:
+
+        @pl.when(when)
+        def _():
+            ahead_copy(0, choice).wait_send()
+            ahead_copy(1, choice).wait_send()
+
     for side in range(8):
 
         @pl.when(inside(*AROUND[side]))
         def _():
-            for image in (LEFT, RIGHT):
-                halo_copy(side, image).wait_send()
+            halo_copy(side, pl.ds(0, 2)).wait_send()
+
+    finish(chunks - 1, held)
+
+    @pl.when(odd & has_two)
+    def _():
+        sent(far, near, 1, 0, -1).wait_send()
+
+    @pl.when(even & gives_two)
+    def _():
+        sent(tri_out, tri_in, 2, 0, 2).wait_send()
+
+
+def store_kernel(batch, height, part, span_count, level_count, scale, done, held, out, tail, stage, sems):
+    edge = part // 2
+    last = (batch - 1) * height
+    pieces = [(b * height + h, part) for b in range(batch - 1) for h in range(0, height, part)]
+    pieces += [(last + h, part) for h in range(edge, height - edge, part)]
+    copies = []
+    for start, size in pieces:
+        rows = pl.ds(start, size)
+        copies.append(pltpu.make_async_copy(done.at[rows], out.at[rows], sems.at[len(copies)]))
+    for copy in copies:
+        copy.start()
+    for half, start in enumerate((last, last + height - edge)):
+        for row in range(half * edge, half * edge + edge):
+            volume_row(held, stage, tail, row, row, span_count, level_count, scale)
+        copies.append(
+            pltpu.make_async_copy(
+                tail.at[pl.ds(half * edge, edge)], out.at[pl.ds(start, edge)], sems.at[len(copies)]
+            )
+        )
+        copies[-1].start()
+    for copy in copies:
+        copy.wait()
 
 
 def in_hbm(array):
@@ -467,19 +562,24 @@
     dma = pltpu.SemaphoreType.DMA
     bf16, f32 = jnp.bfloat16, jnp.float32
     tri = (lines // 2, breadth // 16 + 1, 16, breadth)
-    out = pl.pallas_call(
+    stage = pltpu.VMEM((part, 3, DISP + 16, breadth), f32)
+    scale = 1.0 / math.sqrt(channels)
+    done, held = pl.pallas_call(
         functools.partial(
-            kernel, lax.axis_size("rows"), col_count, part, DISP, LEVELS, 1.0 / math.sqrt(channels)
+            kernel, lax.axis_size("rows"), col_count, part, DISP, LEVELS, scale
         ),
-        out_shape=jax.ShapeDtypeStruct((lines, width, breadth), f32),
+        out_shape=[
+            jax.ShapeDtypeStruct((lines, width, breadth), f32),
+            jax.ShapeDtypeStruct((part, 3 * breadth, breadth), f32),
+        ],
         in_specs=[hbm] * 4,
-        out_specs=vmem,
+        out_specs=[vmem] * 2,
         scratch_shapes=[
-            pltpu.VMEM((2, batch, height + 2, breadth, channels), bf16),
+            pltpu.VMEM((3, batch, height + 2, breadth, channels), bf16),
             pltpu.VMEM((part + 4, breadth, 2 * channels), bf16),
             pltpu.VMEM((2, 2, batch, height, 16, channels), bf16),
             pltpu.VMEM((2, 2, batch, height, 1, channels), f32),
-            pltpu.VMEM((2, 2, batch, height + 2, 1, channels), f32),
+            pltpu.VMEM((2, 3, batch, height + 2, 1, channels), f32),
             pltpu.VMEM((9 * channels, channels), bf16),
             pltpu.VMEM((1, channels), f32),
             pltpu.VMEM((2, lines, breadth, channels), bf16),
@@ -489,9 +589,9 @@
             pltpu.VMEM(tri, bf16),
             pltpu.VMEM(tri, bf16),
             pltpu.VMEM((part, 3 * breadth, breadth), f32),
-            pltpu.VMEM((part, 3, DISP + 16, breadth), f32),
-            dma((4,)), dma((2, 2)), dma((2, 8)), dma((2, 8)),
-            dma((2, chunks)), dma((2, chunks)), dma((2, chunks)), dma((2, chunks)), dma((2, chunks)),
+            stage,
+            dma((4,)), dma((2, 2)), dma((8,)), dma((2, 8)), dma((2, 2)),
+            dma((3,)), dma((chunks,)), dma((chunks,)), dma((chunks,)),
         ],
         compiler_params=pltpu.CompilerParams(
             collective_id=0, has_side_effects=True, vmem_limit_bytes=40 * 2**20
@@ -500,6 +600,16 @@
         in_hbm(left_features), in_hbm(right_features),
         in_hbm(conv_weight.reshape(9 * channels, channels)), in_hbm(conv_bias.reshape(1, -1)),
     )
+    out = pl.pallas_call(
+        functools.partial(store_kernel, batch, height, part, DISP, LEVELS, scale),
+        out_shape=jax.ShapeDtypeStruct((lines, width, breadth), f32),
+        in_specs=[vmem] * 2,
+        out_specs=hbm,
+        scratch_shapes=[
+            pltpu.VMEM((part, width, breadth), f32), stage, dma((chunks + 1,)),
+        ],
+        compiler_params=pltpu.CompilerParams(vmem_limit_bytes=8 * 2**20),
+    )(done, held)
     return jnp.swapaxes(out, 1, 2).reshape(batch, height, breadth, -1)
 
 

time: 35.2 us -> 32.5 us (0.923)
  local copies, waits for them, and re-layouts: 2.58 us -> 0 us
    pallas_call x1, Pallas kernels: 32.5 us -> 29.6 us  [shards(): pl.pallas_call(functools.partial(kernel, lax.axis_size('rows'), col_count...]
    pallas_call x0 -> x1, Pallas kernels: none -> 2.61 us  [shards(): pl.pallas_call(functools.partial(store_kernel, batch, height, part, DISP,...]
    unnamed x1 -> x0, local copies, waits for them, and re-layouts: 2.58 us -> none
where the time goes in v3:
time: 32.5 us; the launch traced here: 32.3 us
  Pallas kernels  32.3 us (99%)
    pallas_call x1, Pallas kernels, shards(): pl.pallas_call(functools.partial(kernel, lax.axis_size('rows'), col_count...  29.6 us
    pallas_call x1, Pallas kernels, shards(): pl.pallas_call(functools.partial(store_kernel, batch, height, part, DISP,...  2.61 us

profile of v3, /device:TPU:12, one launch (start us, length us, event | category | flops | bytes accessed | tf_op | source)
XLA Modules:
  0.0 32.3 jit_solution(17701162452258551939)
XLA Ops:
  0.0 29.6 %shard_map.46 = (f32[24,480,128]{2,1,0:T(8,128)S(1)}, f32[4,384,128]{2,1,0:T(8,128)S(1)}) custom-call(bf16[2,12,128,256]{3,2,1,0:T(8,128)(2,1)} %left.1, bf16[2,12,128,256]{3,2,1,0:T(8,128)(2,1)} %right.1, bf16[2304,256]{1,0:T(8,128)(2,1)} %bitcast.5, f32[1,256]{1,0:T(1,128)} %bitcast.6), custom_call_target="tpu_custom_call" | custom-call | tf_op jit(solution)/shard_map/pallas_call | solution.py:567
  29.7 2.6 %shard_map.47 = f32[24,480,128]{2,1,0:T(8,128)} custom-call(f32[24,480,128]{2,1,0:T(8,128)S(1)} %get-tuple-element.7.done, f32[4,384,128]{2,1,0:T(8,128)S(1)} %get-tuple-element.8.held), custom_call_target="tpu_custom_call" | custom-call | tf_op jit(solution)/shard_map/pallas_call | solution.py:603

commit v4 on v3

--- a/solution.py
+++ b/solution.py
@@ -18,7 +18,8 @@
 ROW_SIDES = (0, 1)
 COL_SIDES = (2, 3)
 CORNERS = (4, 5, 6, 7)
-LEFT, RIGHT, AHEAD = 0, 1, 2
+LEFT, RIGHT = 0, 1
+RIM = 16
 
 
 def volume_row(scores, stage, out, slot, line, span_count, level_count, scale):
@@ -52,8 +53,8 @@
 def kernel(
     row_count, col_count, part, span_count, level_count, scale,
     left, right, weight_hbm, bias_hbm, out, held,
-    images, sides, raw_edges, edges, col_halo, weight, bias, enc, near, far, back, tri_out, tri_in, scores, stage,
-    in_sems, edge_sems, halo_sems, recv_sem, ahead_sems, send_sems, near_sems, two_sems, back_sems,
+    images, sides, raw_edges, edges, col_halo, weight, bias, enc, early, near, far, back, tri_out, tri_in, scores, stage,
+    in_sems, edge_sems, halo_sems, recv_sem, early_sems, rim_sems, send_sems, near_sems, two_sems, back_sems, go_sem,
 ):
     batch, height, breadth, channels = left.shape
     my_row, my_col = lax.axis_index("rows"), lax.axis_index("cols")
@@ -61,6 +62,7 @@
     spans = height // part - 1
     chunks = batch * (spans + 1)
     inner = batch * spans
+    ahead = min(inner, 2)
 
     def inside(step_row, step_col):
         row, col = my_row + step_row, my_col + step_col
@@ -135,28 +137,7 @@
             device_id=(my_row + step_row, my_col + step_col), device_id_type=MESH,
         )
 
-    def ahead_copy(which, image):
-        lines = pl.ds(edge, part + 2)
-        if which == 0:
-            source, target = images.at[image, 0, lines], images.at[AHEAD, 0, lines]
-        else:
-            source, target = col_halo.at[:, image, 0, lines], col_halo.at[:, AHEAD, 0, lines]
-        return pltpu.make_async_remote_copy(
-            src_ref=source, dst_ref=target,
-            send_sem=ahead_sems.at[0, which], recv_sem=ahead_sems.at[1, which],
-            device_id=(my_row, my_col + (2 if image == RIGHT else -2)), device_id_type=MESH,
-        )
-
-    sends_ahead = ((RIGHT, odd & gives_two), (LEFT, even & has_two))
-    takes_ahead = ((RIGHT, odd & has_two), (LEFT, even & gives_two))
-
-    def send_ahead(which, image):
-        for choice, when in sends_ahead:
-            if choice == image:
-
-                @pl.when(when)
-                def _():
-                    ahead_copy(which, choice).start()
+    sends_early = ((RIGHT, odd & gives_two), (LEFT, even & has_two))
 
     def take_edges(image):
         for b in range(batch):
@@ -223,10 +204,8 @@
         def _():
             send_halo(COL_SIDES + CORNERS, 1 - image)
             fetch(image).wait()
-            send_ahead(0, image)
             send_halo(ROW_SIDES, image)
             fetch(1 - image).wait()
-            send_ahead(0, 1 - image)
             send_halo(ROW_SIDES, 1 - image)
 
     clear_halo()
@@ -273,7 +252,7 @@
         return remote(enc.at[RIGHT], near, 0, near_sems, step, 1)
 
     def far_copy(step):
-        return remote(enc.at[RIGHT], far, 0, two_sems, step, 2)
+        return remote(enc.at[RIGHT], far, jnp.where(step == chunks - 1, 3, 0), two_sems, step, 2)
 
     def pass_copy(step):
         return remote(far, near, 1, near_sems, step, -1)
@@ -282,23 +261,78 @@
         return remote(enc.at[LEFT], back, 1, back_sems, step, -2)
 
     def tri_copy(step):
-        return remote(tri_out, tri_in, 2, two_sems, step, 2, part // 2)
-
-    def sent(source, target, send, first_line, away):
-        lines = pl.ds(first_line, source.shape[0] - first_line)
+        return remote(tri_out, tri_in, 2, two_sems, step, 2, 1)
+
+    def toward_two(image):
+        return (far, my_col + 2) if image == RIGHT else (back, my_col - 2)
+
+    def early_copy(piece, image):
+        target, col = toward_two(image)
+        lines, pixels = pl.ds(piece * edge, edge), pl.ds(RIM, breadth - 2 * RIM)
+        return pltpu.make_async_remote_copy(
+            src_ref=early.at[lines, pixels], dst_ref=target.at[lines, pixels],
+            send_sem=send_sems.at[4], recv_sem=early_sems.at[piece],
+            device_id=(my_row, col), device_id_type=MESH,
+        )
+
+    def rim_copy(step, side, image):
+        target, col = toward_two(image)
+        lines, pixels = pl.ds(step * part, part), pl.ds(side * (breadth - RIM), RIM)
+        return pltpu.make_async_remote_copy(
+            src_ref=enc.at[image, lines, pixels], dst_ref=target.at[lines, pixels],
+            send_sem=send_sems.at[5], recv_sem=rim_sems.at[2 * step + side],
+            device_id=(my_row, col), device_id_type=MESH,
+        )
+
+    def wait_two(step, image):
+        @pl.when(step < ahead)
+        def _():
+            for half in range(2):
+                early_copy(2 * step + half, image).wait_recv()
+                rim_copy(step, half, image).wait_recv()
+
+        @pl.when(step >= ahead)
+        def _():
+            (far_copy if image == RIGHT else back_copy)(step).wait_recv()
+
+    def start_two(step, image):
+        @pl.when(step < ahead)
+        def _():
+            for side in range(2):
+                rim_copy(step, side, image).start()
+
+        @pl.when(step >= ahead)
+        def _():
+            (far_copy if image == RIGHT else back_copy)(step).start()
+
+    def sent_early(image):
+        target, col = toward_two(image)
+        lines = pl.ds(0, ahead * part)
+        for send, source, pixels in (
+            (4, early, pl.ds(RIM, breadth - 2 * RIM)), (5, enc.at[image], pl.ds(0, 2 * RIM))
+        ):
+            yield pltpu.make_async_remote_copy(
+                src_ref=source.at[lines, pixels], dst_ref=target.at[lines, pixels],
+                send_sem=send_sems.at[send], recv_sem=near_sems.at[0],
+                device_id=(my_row, col), device_id_type=MESH,
+            )
+
+    def sent(source, target, send, away, low=0, high=chunks, rows=part):
+        lines = pl.ds(low * rows, (high - low) * rows)
         return pltpu.make_async_remote_copy(
             src_ref=source.at[lines], dst_ref=target.at[lines],
             send_sem=send_sems.at[send], recv_sem=near_sems.at[0],
             device_id=(my_row, my_col + away), device_id_type=MESH,
         )
 
-    def convolve(image, step, b, starts, count):
+    def encoded(image, b, starts, count, bare):
         slots = count + 2
+        rows = count * len(starts)
         for piece, start in enumerate(starts):
             for line in range(slots):
                 row = images[image, b, start + line].astype(jnp.float32)
-                before = col_halo[0, image, b, start + line]
-                after = col_halo[1, image, b, start + line]
+                before = 0.0 if bare else col_halo[0, image, b, start + line]
+                after = 0.0 if bare else col_halo[1, image, b, start + line]
                 sides[piece * slots + line, :, :channels] = jnp.where(
                     column == 0, before, pltpu.roll(row, 1, 0)
                 ).astype(jnp.bfloat16)
@@ -308,61 +342,73 @@
 
         def rows_from(offset):
             taken = [images[image, b, pl.ds(start + offset, count)] for start in starts]
-            return jnp.concatenate(taken, axis=0).reshape(part * breadth, channels)
+            return jnp.concatenate(taken, axis=0).reshape(rows * breadth, channels)
 
         pieces = []
         for tap in range(3):
             beside = jnp.concatenate(
                 [sides[i * slots + tap : i * slots + tap + count] for i in range(len(starts))], axis=0
-            ).reshape(part * breadth, 2 * channels)
+            ).reshape(rows * breadth, 2 * channels)
             pieces += [beside[:, :channels], rows_from(tap), beside[:, channels:]]
         total = jnp.dot(
             jnp.concatenate(pieces, axis=1), weight[...], preferred_element_type=jnp.float32
         ) + bias[...]
         result = rows_from(1).astype(jnp.float32) + jnp.maximum(total, 0.0)
-        result = result.astype(jnp.bfloat16).reshape(part, breadth, channels)
+        return result.astype(jnp.bfloat16).reshape(rows, breadth, channels)
+
+    def turned(plain):
+        return jnp.dot(flip, plain, preferred_element_type=jnp.float32).astype(jnp.bfloat16)
+
+    def convolve(image, step, b, starts, count):
+        result = encoded(image, b, starts, count, False)
         base = step * part
 
         @pl.when(image == LEFT)
         def _():
             enc[LEFT, pl.ds(base, part)] = result
 
-            @pl.when(even & has_two & (step > 0))
+            @pl.when(even & has_two)
             def _():
-                back_copy(step).start()
-
-        def turned(row):
-            return jnp.dot(flip, result[row], preferred_element_type=jnp.float32).astype(jnp.bfloat16)
-
-        @pl.when((image == AHEAD) & odd)
+                start_two(step, LEFT)
+
+        @pl.when(image == RIGHT)
         def _():
             for row in range(part):
-                far[base + row] = turned(row)
-            pass_copy(step).start()
-
-        @pl.when((image == AHEAD) & even)
-        def _():
-            back[pl.ds(base, part)] = result
-
-        @pl.when(image == RIGHT)
-        def _():
-            for row in range(part):
-                enc[RIGHT, base + row] = turned(row)
+                enc[RIGHT, base + row] = turned(result[row])
 
             @pl.when(even)
             def _():
                 own_copy(step).start()
 
-            @pl.when(odd & gives_two & (step > 0))
+            @pl.when(odd & gives_two)
             def _():
-                far_copy(step).start()
-
-    def conv_inner(image, low, high):
+                start_two(step, RIGHT)
+
+    def conv_early(piece, carry):
+        step = piece // 2
+        start = edge + lax.rem(step, spans) * part + lax.rem(piece, 2) * edge
+        image = jnp.where(odd, RIGHT, LEFT)
+        result = encoded(image, step // spans, [start], edge, True)
+
+        @pl.when(odd)
+        def _():
+            for row in range(edge):
+                early[piece * edge + row] = turned(result[row])
+            early_copy(piece, RIGHT).start()
+
+        @pl.when(even)
+        def _():
+            early[pl.ds(piece * edge, edge)] = result
+            early_copy(piece, LEFT).start()
+
+        return carry
+
+    def conv_inner(image):
         def body(step, carry):
             convolve(image, step, step // spans, [edge + lax.rem(step, spans) * part], part)
             return carry
 
-        lax.fori_loop(low, high, body, 0)
+        lax.fori_loop(0, inner, body, 0)
 
     def conv_edge(image):
         def body(step, carry):
@@ -388,22 +434,55 @@
 
     def triangle(step, carry):
         base = step * part
-
-        @pl.when(step > 0)
-        def _():
-            back_copy(step).wait_recv()
-
-        for pair in range(0, part, 2):
-            two = [product(enc[RIGHT, base + row], back[base + row]) for row in (pair, pair + 1)]
-            for i in range(half_blocks + 1):
+        wait_two(step, LEFT)
+        packed, middles = [], []
+        for row in range(part):
+            block = product(enc[RIGHT, base + row], back[base + row])
+            packed.append(block[0:8])
+            for i in range(1, half_blocks):
                 cut = breadth - 8 * i
-                kept = []
-                for block in two:
-                    piece = block[8 * i : 8 * i + 8]
-                    if 0 < i < half_blocks:
-                        piece = jnp.where(lane8 < cut, piece, pltpu.roll(block[cut : cut + 8], cut, 1))
-                    kept.append(piece)
-                tri_out[(base + pair) // 2, i] = jnp.concatenate(kept, axis=0).astype(jnp.bfloat16)
+                packed.append(
+                    jnp.where(
+                        lane8 < cut, block[8 * i : 8 * i + 8], pltpu.roll(block[cut : cut + 8], cut, 1)
+                    )
+                )
+            middles.append(block[8 * half_blocks : 8 * half_blocks + 8])
+        for row in range(0, part, 2):
+            packed.append(
+                jnp.where(
+                    lane8 < breadth // 2, middles[row], pltpu.roll(middles[row + 1], breadth // 2, 1)
+                )
+            )
+        packed += packed[: len(packed) % 2]
+        for i in range(len(packed) // 2):
+            tile = jnp.concatenate(packed[2 * i : 2 * i + 2], axis=0)
+            tri_out[step, i] = tile.astype(jnp.bfloat16)
+
+        @pl.when(step >= inner)
+        def _():
+            tri_copy(step).start()
+
+        return carry
+
+    def unpack_triangle(step, scores):
+        def packed(index):
+            tile = tri_in[step, index // 2].astype(jnp.float32)
+            return tile[8 * (index % 2) : 8 * (index % 2) + 8]
+
+        def put(row, block_row, block):
+            start = 2 * breadth + 8 * block_row
+            scores[row, start : start + 8] = block
+
+        for row in range(part):
+            for i in range(half_blocks):
+                block = packed(row * half_blocks + i)
+                put(row, i, block)
+                if i > 0:
+                    put(row, 2 * half_blocks - i, pltpu.roll(block, 8 * i, 1))
+            block = packed(part * half_blocks + row // 2)
+            put(row, half_blocks, block if row % 2 == 0 else pltpu.roll(block, breadth // 2, 1))
+
+    def send_triangle(step, carry):
         tri_copy(step).start()
         return carry
 
@@ -412,28 +491,27 @@
         def _():
             lax.fori_loop(low, high, triangle, 0)
 
+    @pl.when((odd & gives_two) | (even & has_two))
+    def _():
+        lax.fori_loop(0, 2 * ahead, conv_early, 0)
+
     both(functools.partial(wait_halo, COL_SIDES), first)
-
-    both(functools.partial(send_ahead, 1), first)
-    conv_inner(first, 0, inner)
+    conv_inner(first)
     both(functools.partial(wait_halo, COL_SIDES), second)
-    both(functools.partial(send_ahead, 1), second)
-    conv_inner(second, 0, inner)
-    for choice, when in takes_ahead:
-
-        @pl.when(when)
-        def _():
-            ahead_copy(0, choice).wait_recv()
-            ahead_copy(1, choice).wait_recv()
-
-    any_ahead = (odd & has_two) | (even & gives_two)
-    conv_inner(AHEAD, 0, jnp.where(any_ahead, 1, 0))
+    conv_inner(second)
     both(functools.partial(wait_halo, ROW_SIDES + CORNERS), first)
     conv_edge(first)
     triangles(0, inner)
     both(functools.partial(wait_halo, ROW_SIDES + CORNERS), second)
     conv_edge(second)
+
+    @pl.when(even & gives_two)
+    def _():
+        pl.semaphore_wait(go_sem, 1)
+        lax.fori_loop(0, inner, send_triangle, 0)
+
     triangles(inner, chunks)
+
 
     def finish(step, scores):
         base = step * part
@@ -444,11 +522,8 @@
 
         @pl.when(odd & has_two)
         def _():
-            @pl.when(step > 0)
-            def _():
-                far_copy(step).wait_recv()
-                pass_copy(step).start()
-
+            wait_two(step, RIGHT)
+            pass_copy(step).start()
             for row in range(part):
                 scores[row, 2 * breadth : 3 * breadth] = product(
                     far[base + row], enc[LEFT, base + row]
@@ -457,18 +532,15 @@
         @pl.when(even & has_two)
         def _():
             pass_copy(step).wait_recv()
-            tri_copy(step).wait_recv()
-            for pair in range(0, part, 2):
-                for i in range(half_blocks + 1):
-                    both_rows = tri_in[(base + pair) // 2, i].astype(jnp.float32)
-                    for row in range(2):
-                        block = both_rows[8 * row : 8 * row + 8]
-                        start = 2 * breadth + 8 * i
-                        scores[pair + row, start : start + 8] = block
-                        if 0 < i < half_blocks:
-                            start = 3 * breadth - 8 * i
-                            scores[pair + row, start : start + 8] = pltpu.roll(block, 8 * i, 1)
-
+
+        def take_triangle():
+            @pl.when(even & has_two)
+            def _():
+                tri_copy(step).wait_recv()
+                unpack_triangle(step, scores)
+
+        if scores is not held:
+            take_triangle()
         for row in range(part):
             scores[row, :breadth] = product(enc[RIGHT, base + row], enc[LEFT, base + row])
             scores[row, breadth : 2 * breadth] = product(near[base + row], enc[LEFT, base + row])
@@ -477,6 +549,8 @@
                 volume_row(
                     scores, stage, out, row, b * height + h, span_count, level_count, scale
                 )
+        if scores is held:
+            take_triangle()
 
     def finish_one(step, carry):
         finish(step, scores)
@@ -484,40 +558,45 @@
 
     lax.fori_loop(0, chunks - 1, finish_one, 0)
 
+    @pl.when(odd & gives_two)
+    def _():
+        sent(enc.at[RIGHT], far, 0, 2, ahead, chunks - 1).wait_send()
+        pl.semaphore_signal(go_sem, inc=1, device_id=(my_row, my_col - 1), device_id_type=MESH)
+
     @pl.when(even)
     def _():
-        sent(enc.at[RIGHT], near, 0, 0, 1).wait_send()
+        sent(enc.at[RIGHT], near, 0, 1).wait_send()
 
     @pl.when(even & has_two)
     def _():
-        sent(enc.at[LEFT], back, 1, part, -2).wait_send()
+        sent(enc.at[LEFT], back, 1, -2, ahead).wait_send()
+
+    for choice, when in sends_early:
+
+        @pl.when(when)
+        def _():
+            for copy in sent_early(choice):
+                copy.wait_send()
+
+    for side in range(8):
+
+        @pl.when(inside(*AROUND[side]))
+        def _():
+            halo_copy(side, pl.ds(0, 2)).wait_send()
+
+    finish(chunks - 1, held)
+
+    @pl.when(odd & has_two)
+    def _():
+        sent(far, near, 1, -1).wait_send()
+
+    @pl.when(even & gives_two)
+    def _():
+        sent(tri_out, tri_in, 2, 2, rows=1).wait_send()
 
     @pl.when(odd & gives_two)
     def _():
-        sent(enc.at[RIGHT], far, 0, part, 2).wait_send()
-
-    for choice, when in sends_ahead:
-
-        @pl.when(when)
-        def _():
-            ahead_copy(0, choice).wait_send()
-            ahead_copy(1, choice).wait_send()
-
-    for side in range(8):
-
-        @pl.when(inside(*AROUND[side]))
-        def _():
-            halo_copy(side, pl.ds(0, 2)).wait_send()
-
-    finish(chunks - 1, held)
-
-    @pl.when(odd & has_two)
-    def _():
-        sent(far, near, 1, 0, -1).wait_send()
-
-    @pl.when(even & gives_two)
-    def _():
-        sent(tri_out, tri_in, 2, 0, 2).wait_send()
+        sent(enc.at[RIGHT], far, 3, 2, chunks - 1).wait_send()
 
 
 def store_kernel(batch, height, part, span_count, level_count, scale, done, held, out, tail, stage, sems):
@@ -552,16 +631,17 @@
     batch, height, breadth, channels = left_features.shape
     col_count = lax.axis_size("cols")
     part = math.gcd(height, 4)
-    assert 2 * breadth == DISP and col_count % 2 == 0 and breadth % 16 == 0
+    assert 2 * breadth == DISP and col_count % 2 == 0 and breadth % 32 == 0
     assert part % 2 == 0 and height > part
     lines = batch * height
     chunks = lines // part
+    ahead = min(chunks - batch, 2)
     width = sum(DISP >> level for level in range(LEVELS))
     hbm = pl.BlockSpec(memory_space=pltpu.HBM)
     vmem = pl.BlockSpec(memory_space=pltpu.VMEM)
     dma = pltpu.SemaphoreType.DMA
     bf16, f32 = jnp.bfloat16, jnp.float32
-    tri = (lines // 2, breadth // 16 + 1, 16, breadth)
+    tri = (chunks, pl.cdiv(part * (breadth // 16) + part // 2, 2), 16, breadth)
     stage = pltpu.VMEM((part, 3, DISP + 16, breadth), f32)
     scale = 1.0 / math.sqrt(channels)
     done, held = pl.pallas_call(
@@ -575,14 +655,15 @@
         in_specs=[hbm] * 4,
         out_specs=[vmem] * 2,
         scratch_shapes=[
-            pltpu.VMEM((3, batch, height + 2, breadth, channels), bf16),
+            pltpu.VMEM((2, batch, height + 2, breadth, channels), bf16),
             pltpu.VMEM((part + 4, breadth, 2 * channels), bf16),
             pltpu.VMEM((2, 2, batch, height, 16, channels), bf16),
             pltpu.VMEM((2, 2, batch, height, 1, channels), f32),
-            pltpu.VMEM((2, 3, batch, height + 2, 1, channels), f32),
+            pltpu.VMEM((2, 2, batch, height + 2, 1, channels), f32),
             pltpu.VMEM((9 * channels, channels), bf16),
             pltpu.VMEM((1, channels), f32),
             pltpu.VMEM((2, lines, breadth, channels), bf16),
+            pltpu.VMEM((ahead * part, breadth, channels), bf16),
             pltpu.VMEM((lines, breadth, channels), bf16),
             pltpu.VMEM((lines, breadth, channels), bf16),
             pltpu.VMEM((lines, breadth, channels), bf16),
@@ -590,8 +671,8 @@
             pltpu.VMEM(tri, bf16),
             pltpu.VMEM((part, 3 * breadth, breadth), f32),
             stage,
-            dma((4,)), dma((2, 2)), dma((8,)), dma((2, 8)), dma((2, 2)),
-            dma((3,)), dma((chunks,)), dma((chunks,)), dma((chunks,)),
+            dma((4,)), dma((2, 2)), dma((8,)), dma((2, 8)), dma((2 * ahead,)), dma((2 * ahead,)),
+            dma((6,)), dma((chunks,)), dma((chunks,)), dma((chunks,)), pltpu.SemaphoreType.REGULAR,
         ],
         compiler_params=pltpu.CompilerParams(
             collective_id=0, has_side_effects=True, vmem_limit_bytes=40 * 2**20

time: 32.5 us -> 31.2 us (0.960)
  Pallas kernels: 32.3 us -> 30.8 us
    pallas_call x1, Pallas kernels: 29.6 us -> 28.2 us  [shards(): pl.pallas_call(functools.partial(kernel, lax.axis_size('rows'), col_count...]
where the time goes in v4:
time: 31.2 us; the launch traced here: 30.8 us
  Pallas kernels  30.8 us (99%)
    pallas_call x1, Pallas kernels, shards(): pl.pallas_call(functools.partial(kernel, lax.axis_size('rows'), col_count...  28.2 us
    pallas_call x1, Pallas kernels, shards(): pl.pallas_call(functools.partial(store_kernel, batch, height, part, DISP,...  2.61 us

profile of v4, /device:TPU:12, one launch (start us, length us, event | category | flops | bytes accessed | tf_op | source)
XLA Modules:
  0.0 30.8 jit_solution(4223408070970597003)
XLA Ops:
  0.0 28.2 %shard_map.46 = (f32[24,480,128]{2,1,0:T(8,128)S(1)}, f32[4,384,128]{2,1,0:T(8,128)S(1)}) custom-call(bf16[2,12,128,256]{3,2,1,0:T(8,128)(2,1)} %left.1, bf16[2,12,128,256]{3,2,1,0:T(8,128)(2,1)} %right.1, bf16[2304,256]{1,0:T(8,128)(2,1)} %bitcast.5, f32[1,256]{1,0:T(1,128)} %bitcast.6), custom_call_target="tpu_custom_call" | custom-call | tf_op jit(solution)/shard_map/pallas_call | solution.py:647
  28.2 2.6 %shard_map.47 = f32[24,480,128]{2,1,0:T(8,128)} custom-call(f32[24,480,128]{2,1,0:T(8,128)S(1)} %get-tuple-element.7.done, f32[4,384,128]{2,1,0:T(8,128)S(1)} %get-tuple-element.8.held), custom_call_target="tpu_custom_call" | custom-call | tf_op jit(solution)/shard_map/pallas_call | solution.py:684

commit v5 on v4

--- a/solution.py
+++ b/solution.py
@@ -252,7 +252,7 @@
         return remote(enc.at[RIGHT], near, 0, near_sems, step, 1)
 
     def far_copy(step):
-        return remote(enc.at[RIGHT], far, jnp.where(step == chunks - 1, 3, 0), two_sems, step, 2)
+        return remote(enc.at[RIGHT], far, 0, two_sems, step, 2)
 
     def pass_copy(step):
         return remote(far, near, 1, near_sems, step, -1)
@@ -271,7 +271,7 @@
         lines, pixels = pl.ds(piece * edge, edge), pl.ds(RIM, breadth - 2 * RIM)
         return pltpu.make_async_remote_copy(
             src_ref=early.at[lines, pixels], dst_ref=target.at[lines, pixels],
-            send_sem=send_sems.at[4], recv_sem=early_sems.at[piece],
+            send_sem=send_sems.at[3], recv_sem=early_sems.at[piece // 2],
             device_id=(my_row, col), device_id_type=MESH,
         )
 
@@ -280,16 +280,15 @@
         lines, pixels = pl.ds(step * part, part), pl.ds(side * (breadth - RIM), RIM)
         return pltpu.make_async_remote_copy(
             src_ref=enc.at[image, lines, pixels], dst_ref=target.at[lines, pixels],
-            send_sem=send_sems.at[5], recv_sem=rim_sems.at[2 * step + side],
+            send_sem=send_sems.at[4], recv_sem=rim_sems.at[step],
             device_id=(my_row, col), device_id_type=MESH,
         )
 
     def wait_two(step, image):
         @pl.when(step < ahead)
         def _():
-            for half in range(2):
-                early_copy(2 * step + half, image).wait_recv()
-                rim_copy(step, half, image).wait_recv()
+            for copy in arrived_early(step, image):
+                copy.wait_recv()
 
         @pl.when(step >= ahead)
         def _():
@@ -305,17 +304,24 @@
         def _():
             (far_copy if image == RIGHT else back_copy)(step).start()
 
-    def sent_early(image):
+    def pieces_of(first_step, steps, image):
         target, col = toward_two(image)
-        lines = pl.ds(0, ahead * part)
-        for send, source, pixels in (
-            (4, early, pl.ds(RIM, breadth - 2 * RIM)), (5, enc.at[image], pl.ds(0, 2 * RIM))
+        lines = pl.ds(first_step * part, steps * part)
+        for send, recv, source, pixels in (
+            (3, early_sems, early, pl.ds(RIM, breadth - 2 * RIM)),
+            (4, rim_sems, enc.at[image], pl.ds(0, 2 * RIM)),
         ):
             yield pltpu.make_async_remote_copy(
                 src_ref=source.at[lines, pixels], dst_ref=target.at[lines, pixels],
-                send_sem=send_sems.at[send], recv_sem=near_sems.at[0],
+                send_sem=send_sems.at[send], recv_sem=recv.at[first_step],
                 device_id=(my_row, col), device_id_type=MESH,
             )
+
+    def arrived_early(step, image):
+        return pieces_of(jnp.minimum(step, ahead - 1), 1, image)
+
+    def sent_early(image):
+        return pieces_of(0, ahead, image)
 
     def sent(source, target, send, away, low=0, high=chunks, rows=part):
         lines = pl.ds(low * rows, (high - low) * rows)
@@ -505,12 +511,14 @@
     both(functools.partial(wait_halo, ROW_SIDES + CORNERS), second)
     conv_edge(second)
 
+    @pl.when(odd & gives_two)
+    def _():
+        pl.semaphore_signal(go_sem, inc=1, device_id=(my_row, my_col - 1), device_id_type=MESH)
+
     @pl.when(even & gives_two)
     def _():
         pl.semaphore_wait(go_sem, 1)
         lax.fori_loop(0, inner, send_triangle, 0)
-
-    triangles(inner, chunks)
 
 
     def finish(step, scores):
@@ -556,12 +564,9 @@
         finish(step, scores)
         return carry
 
-    lax.fori_loop(0, chunks - 1, finish_one, 0)
-
-    @pl.when(odd & gives_two)
-    def _():
-        sent(enc.at[RIGHT], far, 0, 2, ahead, chunks - 1).wait_send()
-        pl.semaphore_signal(go_sem, inc=1, device_id=(my_row, my_col - 1), device_id_type=MESH)
+    lax.fori_loop(0, inner, finish_one, 0)
+    triangles(inner, chunks)
+    lax.fori_loop(inner, chunks - 1, finish_one, 0)
 
     @pl.when(even)
     def _():
@@ -596,7 +601,7 @@
 
     @pl.when(odd & gives_two)
     def _():
-        sent(enc.at[RIGHT], far, 3, 2, chunks - 1).wait_send()
+        sent(enc.at[RIGHT], far, 0, 2, ahead).wait_send()
 
 
 def store_kernel(batch, height, part, span_count, level_count, scale, done, held, out, tail, stage, sems):
@@ -671,8 +676,8 @@
             pltpu.VMEM(tri, bf16),
             pltpu.VMEM((part, 3 * breadth, breadth), f32),
             stage,
-            dma((4,)), dma((2, 2)), dma((8,)), dma((2, 8)), dma((2 * ahead,)), dma((2 * ahead,)),
-            dma((6,)), dma((chunks,)), dma((chunks,)), dma((chunks,)), pltpu.SemaphoreType.REGULAR,
+            dma((4,)), dma((2, 2)), dma((8,)), dma((2, 8)), dma((ahead,)), dma((ahead,)),
+            dma((5,)), dma((chunks,)), dma((chunks,)), dma((chunks,)), pltpu.SemaphoreType.REGULAR,
         ],
         compiler_params=pltpu.CompilerParams(
             collective_id=0, has_side_effects=True, vmem_limit_bytes=40 * 2**20

time: 31.2 us -> 30 us (0.962)
  Pallas kernels: 30.8 us -> 29.6 us
    pallas_call x1, Pallas kernels: 28.2 us -> 27 us  [shards(): pl.pallas_call(functools.partial(kernel, lax.axis_size('rows'), col_count...]
where the time goes in v5:
time: 30 us; the launch traced here: 29.7 us
  Pallas kernels  29.6 us (99%)
    pallas_call x1, Pallas kernels, shards(): pl.pallas_call(functools.partial(kernel, lax.axis_size('rows'), col_count...  27 us
    pallas_call x1, Pallas kernels, shards(): pl.pallas_call(functools.partial(store_kernel, batch, height, part, DISP,...  2.61 us

profile of v5, /device:TPU:12, one launch (start us, length us, event | category | flops | bytes accessed | tf_op | source)
XLA Modules:
  0.0 29.7 jit_solution(14273510448463796634)
XLA Ops:
  0.0 27.0 %shard_map.46 = (f32[24,480,128]{2,1,0:T(8,128)S(1)}, f32[4,384,128]{2,1,0:T(8,128)S(1)}) custom-call(bf16[2,12,128,256]{3,2,1,0:T(8,128)(2,1)} %left.1, bf16[2,12,128,256]{3,2,1,0:T(8,128)(2,1)} %right.1, bf16[2304,256]{1,0:T(8,128)(2,1)} %bitcast.5, f32[1,256]{1,0:T(1,128)} %bitcast.6), custom_call_target="tpu_custom_call" | custom-call | tf_op jit(solution)/shard_map/pallas_call | solution.py:652
  27.0 2.6 %shard_map.47 = f32[24,480,128]{2,1,0:T(8,128)} custom-call(f32[24,480,128]{2,1,0:T(8,128)S(1)} %get-tuple-element.7.done, f32[4,384,128]{2,1,0:T(8,128)S(1)} %get-tuple-element.8.held), custom_call_target="tpu_custom_call" | custom-call | tf_op jit(solution)/shard_map/pallas_call | solution.py:689

commit v6 on v5

--- a/solution.py
+++ b/solution.py
@@ -133,7 +133,7 @@
         return pltpu.make_async_remote_copy(
             src_ref=source, dst_ref=target,
             send_sem=halo_sems.at[side],
-            recv_sem=recv_sem.at[image if isinstance(image, int) else 0, OPPOSITE[side]],
+            recv_sem=recv_sem.at[OPPOSITE[side] + (8 if isinstance(image, int) and image else 0)],
             device_id=(my_row + step_row, my_col + step_col), device_id_type=MESH,
         )
 
@@ -193,7 +193,7 @@
 
         @pl.when(first == image)
         def _():
-            send_halo(COL_SIDES + CORNERS, image)
+            send_halo(COL_SIDES, image)
             for side in range(2):
                 fetch_edge(side, 1 - image).wait()
 
@@ -202,7 +202,8 @@
 
         @pl.when(first == image)
         def _():
-            send_halo(COL_SIDES + CORNERS, 1 - image)
+            send_halo(COL_SIDES, 1 - image)
+            send_halo(CORNERS, pl.ds(0, 2))
             fetch(image).wait()
             send_halo(ROW_SIDES, image)
             fetch(1 - image).wait()
@@ -505,10 +506,11 @@
     conv_inner(first)
     both(functools.partial(wait_halo, COL_SIDES), second)
     conv_inner(second)
-    both(functools.partial(wait_halo, ROW_SIDES + CORNERS), first)
+    both(functools.partial(wait_halo, ROW_SIDES), first)
+    wait_halo(CORNERS, pl.ds(0, 2))
     conv_edge(first)
     triangles(0, inner)
-    both(functools.partial(wait_halo, ROW_SIDES + CORNERS), second)
+    both(functools.partial(wait_halo, ROW_SIDES), second)
     conv_edge(second)
 
     @pl.when(odd & gives_two)
@@ -676,7 +678,7 @@
             pltpu.VMEM(tri, bf16),
             pltpu.VMEM((part, 3 * breadth, breadth), f32),
             stage,
-            dma((4,)), dma((2, 2)), dma((8,)), dma((2, 8)), dma((ahead,)), dma((ahead,)),
+            dma((4,)), dma((2, 2)), dma((8,)), dma((12,)), dma((ahead,)), dma((ahead,)),
             dma((5,)), dma((chunks,)), dma((chunks,)), dma((chunks,)), pltpu.SemaphoreType.REGULAR,
         ],
         compiler_params=pltpu.CompilerParams(

time: 30 us -> 30 us (level)
  no operation moved by 1% of the time
where the time goes in v6:
time: 30 us; the launch traced here: 29.7 us
  Pallas kernels  29.7 us (99%)
    pallas_call x1, Pallas kernels, shards(): pl.pallas_call(functools.partial(kernel, lax.axis_size('rows'), col_count...  27.1 us
    pallas_call x1, Pallas kernels, shards(): pl.pallas_call(functools.partial(store_kernel, batch, height, part, DISP,...  2.61 us

profile of v6, /device:TPU:12, one launch (start us, length us, event | category | flops | bytes accessed | tf_op | source)
XLA Modules:
  0.0 29.7 jit_solution(14510766474152578465)
XLA Ops:
  0.0 27.1 %shard_map.46 = (f32[24,480,128]{2,1,0:T(8,128)S(1)}, f32[4,384,128]{2,1,0:T(8,128)S(1)}) custom-call(bf16[2,12,128,256]{3,2,1,0:T(8,128)(2,1)} %left.1, bf16[2,12,128,256]{3,2,1,0:T(8,128)(2,1)} %right.1, bf16[2304,256]{1,0:T(8,128)(2,1)} %bitcast.5, f32[1,256]{1,0:T(1,128)} %bitcast.6), custom_call_target="tpu_custom_call" | custom-call | tf_op jit(solution)/shard_map/pallas_call | solution.py:654
  27.1 2.6 %shard_map.47 = f32[24,480,128]{2,1,0:T(8,128)} custom-call(f32[24,480,128]{2,1,0:T(8,128)S(1)} %get-tuple-element.7.done, f32[4,384,128]{2,1,0:T(8,128)S(1)} %get-tuple-element.8.held), custom_call_target="tpu_custom_call" | custom-call | tf_op jit(solution)/shard_map/pallas_call | solution.py:691
